TPU v7x, 32 devices: a whole 2x2x4 slice. The times are simulated.
32 devices in a mesh: groups: 2 (over y), seq: 4 (over z), tp: 2 (over x), ref: 2 (over core).
Axes of the slice: x: 2, y: 2, z: 4, core: 2. Of those that a mesh axis runs over, the one named last changes fastest.
Arguments:
- hidden: bfloat16 [2, 2048, 4096], P('ref', ('groups', 'seq'), 'tp'), parts along dimension 1, may hold values from -6 to 6
- segment_ids: int32 [2048], P(('groups', 'seq')), parts along dimension 0, may hold values from 0 to 3, never falling along the last dimension, each value on 1 to 768 neighbouring positions
- targets: int32 [2048], P(('groups', 'seq')), parts along dimension 0, may hold values from 0 to 4095
- loss_mask: int32 [2048], P(('groups', 'seq')), parts along dimension 0, may hold values from 0 to 1, as said below
- attn_gain: float32 [2, 4096], P('ref'), may hold values from 0.5 to 2
- final_gain: float32 [2, 4096], P('ref'), may hold values from 1 to 4
- w_query: bfloat16 [2, 4096, 2048], P('ref', 'seq', 'tp'), may hold values from -0.125 to 0.125
- w_key: bfloat16 [2, 4096, 1024], P('ref', 'seq', 'tp'), may hold values from -0.125 to 0.125
- w_value: bfloat16 [2, 4096, 1024], P('ref', 'seq', 'tp'), may hold values from -0.09375 to 0.09375
- w_out: bfloat16 [2, 2048, 4096], P('ref', 'tp', 'seq'), may hold values from -0.125 to 0.125
- head: bfloat16 [2, 4096, 4096], P('ref', None, ('seq', 'tp')), may hold values from -0.25784398 to 0.25784398
Outputs:
- logprobs: float32 [2, 2048], P('ref', ('groups', 'seq')), parts along dimension 1
There are 2 independent parts, one for each index of `groups`. A program takes and returns all parts, laid end to end along the dimension named above; an argument that names none is the same for every part. Nothing has to cross between parts.
Inputs may be any that keep to these rules, and one draw needn't show every extreme that they name: `loss_mask`: each aligned block of 256 positions holds 1 to 32 positions with mask 1, and some block holds exactly 32. `segment_ids`: never falling; every rollout number appears; the longest rollout holds exactly 768 positions.
All inputs are finite; a program needn't handle non-finite values.
Results may differ from a plain program's by a relative error of at most 0.0003.
Values may be sent and summed in bfloat16 or wider, within the bound.
A program may use at most 128 MiB of HBM per device.

v0:
```python
import jax
import jax.numpy as jnp
from jax import lax
from jax.sharding import PartitionSpec as P

HEAD_DIM = 128
VOCAB_DEV = 512
WINDOW = 2048
CAP = 32
SEGMENTS = 4


EPS = 1e-05
THETA = 500000.0
FARTHEST = 1073741824


def passed_along(value, axis, by):
    length = lax.axis_size(axis)
    pairs = [(i, i + by) for i in range(length) if 0 <= i + by < length]
    return lax.ppermute(value, axis, pairs)


def joined(part, axis, combine):
    gathered = jax.tree.map(lambda a: lax.all_gather(a, axis), part)

    def take(source):
        return jax.tree.map(lambda a: lax.dynamic_index_in_dim(a, source, 0, False), gathered)

    return lax.fori_loop(
        1, lax.axis_size(axis), lambda source, state: combine(state, take(source)), take(0)
    )


def rms_norm(values, gain):
    return values * lax.rsqrt(jnp.mean(values * values, axis=-1, keepdims=True) + EPS) * gain


def rotate(tensor, offsets):
    half = tensor.shape[-1] // 2
    freq = THETA ** (-(jnp.arange(half, dtype=jnp.float32) * 2.0 / tensor.shape[-1]))
    angle = offsets.astype(jnp.float32)[:, None] * freq[None, :]
    cosine = jnp.cos(angle)[:, None, :]
    sine = jnp.sin(angle)[:, None, :]
    first = tensor[..., :half]
    second = tensor[..., half:]
    return jnp.concatenate(
        [first * cosine - second * sine, second * cosine + first * sine], axis=-1
    )


def combine_stats(left, right):
    top = jnp.maximum(left[0], right[0])
    total = left[1] * jnp.exp(left[0] - top) + right[1] * jnp.exp(right[0] - top)
    return (top, total, left[2] + right[2])


def block_stats(scores, allowed):
    row_peak = jnp.max(scores, axis=-1)
    lifted = jnp.where(allowed[None, None, :, :], jnp.exp(scores - row_peak[..., None]), 0.0)
    return (row_peak, jnp.sum(lifted, axis=-1))


def weighted_values(scores, row_peak, row_total, value_block):
    safe_total = jnp.where(row_total > 0.0, row_total, 1.0)
    weights = (jnp.exp(scores - row_peak[..., None]) / safe_total[..., None]).astype(jnp.bfloat16)
    return jnp.einsum("ngck,knd->cngd", weights, value_block, preferred_element_type=jnp.float32)


def shards(
    hidden,
    segment_ids,
    targets,
    loss_mask,
    attn_gain,
    final_gain,
    w_query,
    w_key,
    w_value,
    w_out,
    head,
):
    tokens = hidden.shape[1]
    seq_index = lax.axis_index("seq")
    base = seq_index * tokens
    position = base + jnp.arange(tokens, dtype=jnp.int32)
    whole = lax.all_gather(hidden[0], "tp", axis=1, tiled=True)
    xfloat = whole.astype(jnp.float32)
    normed = rms_norm(xfloat, attn_gain[0]).astype(jnp.bfloat16)
    labels = jnp.arange(SEGMENTS, dtype=jnp.int32)
    member = segment_ids[None, :] == labels[:, None]
    local_first = jnp.min(jnp.where(member, position[None, :], FARTHEST), axis=1)
    starts = lax.pmin(local_first, "seq")
    token_start = jnp.sum(jnp.where(member, starts[:, None], 0), axis=0)
    offsets = position - token_start
    ranking = jnp.cumsum(loss_mask) - 1
    picks = (loss_mask[None, :] == 1) & (
        ranking[None, :] == jnp.arange(CAP, dtype=jnp.int32)[:, None]
    )
    chooser = picks.astype(jnp.bfloat16)
    normed_rows = jnp.dot(chooser, normed, preferred_element_type=jnp.float32).astype(jnp.bfloat16)
    x_rows = jnp.dot(chooser, whole, preferred_element_type=jnp.float32)
    row_pos = jnp.sum(jnp.where(picks, position[None, :], 0), axis=1)
    row_start = jnp.sum(jnp.where(picks, token_start[None, :], 0), axis=1)
    row_target = jnp.sum(jnp.where(picks, targets[None, :], 0), axis=1)
    places = jnp.stack([row_pos, row_start])
    query_cols = w_query.shape[2]
    key_cols = w_key.shape[2]
    local_heads = query_cols // HEAD_DIM
    local_kv = key_cols // HEAD_DIM
    group = local_heads // local_kv
    score_scale = HEAD_DIM ** (-0.5)
    query = jnp.dot(
        normed_rows,
        lax.all_gather(w_query[0], "seq", axis=0, tiled=True),
        preferred_element_type=jnp.float32,
    )
    keys = jnp.dot(
        normed,
        lax.all_gather(w_key[0], "seq", axis=0, tiled=True),
        preferred_element_type=jnp.float32,
    )
    values = jnp.dot(
        normed,
        lax.all_gather(w_value[0], "seq", axis=0, tiled=True),
        preferred_element_type=jnp.float32,
    )
    query = rotate(query.reshape(CAP, local_heads, HEAD_DIM), row_pos - row_start).astype(
        jnp.bfloat16
    )
    keys = rotate(keys.reshape(tokens, local_kv, HEAD_DIM), offsets).astype(jnp.bfloat16)
    values = values.reshape(tokens, local_kv, HEAD_DIM).astype(jnp.bfloat16)

    def masked_scores(query_rows, bounds, key_block, key_base):
        key_pos = key_base + jnp.arange(key_block.shape[0], dtype=jnp.int32)
        row_at = bounds[0][:, None]
        allowed = (key_pos[None, :] <= row_at) & (row_at - key_pos[None, :] < WINDOW)
        allowed = allowed & (key_pos[None, :] >= bounds[1][:, None])
        grouped = query_rows.reshape(CAP, local_kv, group, HEAD_DIM)
        scores = (
            jnp.einsum("cngd,knd->ngck", grouped, key_block, preferred_element_type=jnp.float32)
            * score_scale
        )
        return (jnp.where(allowed[None, None, :, :], scores, -1e30), allowed)

    reach = min(WINDOW // tokens, lax.axis_size("seq") - 1)
    own_scores, own_allowed = masked_scores(query, places, keys, base)
    row_peak, row_total = block_stats(own_scores, own_allowed)
    visited = []
    for step in range(1, reach + 1):
        guest = passed_along(query, "seq", -step)
        guest_places = passed_along(places, "seq", -step)
        guest_scores, guest_allowed = masked_scores(guest, guest_places, keys, base)
        guest_peak, guest_total = block_stats(guest_scores, guest_allowed)
        returned = passed_along(jnp.stack([guest_peak, guest_total]), "seq", step)
        back_peak = jnp.where(seq_index >= step, returned[0], -1e30)
        merged_peak = jnp.maximum(row_peak, back_peak)
        row_total = row_total * jnp.exp(row_peak - merged_peak) + returned[1] * jnp.exp(
            back_peak - merged_peak
        )
        row_peak = merged_peak
        visited.append(guest_scores)
    attended = weighted_values(own_scores, row_peak, row_total, values)
    for step in range(1, reach + 1):
        guest_stats = passed_along(jnp.stack([row_peak, row_total]), "seq", -step)
        share = weighted_values(visited[step - 1], guest_stats[0], guest_stats[1], values)
        attended = attended + passed_along(share, "seq", step)
    attended = attended.astype(jnp.bfloat16).reshape(CAP, query_cols)
    partial_out = jnp.dot(
        attended,
        lax.all_gather(w_out[0], "seq", axis=1, tiled=True),
        preferred_element_type=jnp.float32,
    )
    summed = lax.psum(partial_out, "tp")
    state = x_rows + summed
    final = rms_norm(state, final_gain[0]).astype(jnp.bfloat16)
    all_rows = lax.all_gather(final, "seq", axis=0, tiled=True)
    all_targets = lax.all_gather(row_target, "seq", axis=0, tiled=True)
    logits = jnp.dot(all_rows, head[0], preferred_element_type=jnp.float32)
    vocab_start = (seq_index * lax.axis_size("tp") + lax.axis_index("tp")) * VOCAB_DEV
    local_top = jnp.max(logits, axis=1)
    local_total = jnp.sum(jnp.exp(logits - local_top[:, None]), axis=1)
    hit = all_targets[:, None] == vocab_start + jnp.arange(VOCAB_DEV, dtype=jnp.int32)[None, :]
    local_target = jnp.sum(jnp.where(hit, logits, 0.0), axis=1)
    merged_top, merged_total, merged_target = joined(
        (local_top, local_total, local_target), ("seq", "tp"), combine_stats
    )
    logp = merged_target - (merged_top + jnp.log(merged_total))
    own = lax.dynamic_slice_in_dim(logp, seq_index * CAP, CAP, 0)
    placed = jnp.sum(jnp.where(picks, own[:, None], 0.0), axis=0)
    return placed[None, :].astype(jnp.float32)


def solution(mesh):
    placed = (
        P("ref", ("groups", "seq"), "tp"),
        P(("groups", "seq")),
        P(("groups", "seq")),
        P(("groups", "seq")),
        P("ref", None),
        P("ref", None),
        P("ref", "seq", "tp"),
        P("ref", "seq", "tp"),
        P("ref", "seq", "tp"),
        P("ref", "tp", "seq"),
        P("ref", None, ("seq", "tp")),
    )
    return jax.shard_map(
        shards, mesh=mesh, in_specs=placed, out_specs=P("ref", ("groups", "seq")), check_vma=False
    )
```

profile of v0, /device:TPU:0, one launch (start us, length us, event | category | flops | bytes accessed | tf_op | source)
XLA Modules:
  0.0 650.0 jit_solution(8386865143074642366)
XLA Ops:
  6.5 0.7 all-gather.20.cloned.1.call-update
  7.3 0.7 all-gather.24.cloned.1.call-update
  8.1 0.7 all-gather.26.cloned.1.call-update
  8.8 0.5 all-gather.22.cloned.1.call-update
  9.4 0.5 all-gather.28.cloned.1.call-update
  10.1 9.9 %pmin.7 = s32[4]{0:T(128)S(1)} all-reduce(s32[4]{0:T(128)S(1)} %select_reduce_fusion.10), channel_id=1, replica_groups=mesh['groups'=2,'seq'=4,'tp'=2,'ref'=2] {'seq'}, use_global_device_ids=true, to_apply=%region_5.6 | all-reduce | flops 4 | bytes 32 | tf_op jit(solution)/shard_map/pmin | solution.py:93
  20.1 0.3 reduce-window.9
  20.9 1.3 collective-permute-start
  22.2 1.3 collective-permute-start.3
  23.5 1.3 collective-permute-start.6
  25.0 0.5 multiply_cosine_fusion
  25.6 0.8 collective-permute-done
  26.4 2.3 collective-permute-done.3
  28.7 3.2 collective-permute-done.6
  32.1 12.6 %all-gather.20.cloned.1.call-done = bf16[1,256,4096]{2,1,0:T(8,128)(2,1)} async-done(((bf16[1,256,2048]{2,1,0:T(8,128)(2,1)}), bf16[1,256,4096]{2,1,0:T(8,128)(2,1)}) %all-gather.20.cloned.1.call-update) | async-done | bytes 2097168 | tf_op jit(solution)/shard_map/all_gather | solution.py:87
  44.7 2.1 fusion.11
  46.8 80.2 %all-gather.24.cloned.1.call-done = bf16[1,4096,512]{2,1,0:T(8,128)(2,1)} async-done(((bf16[1,1024,512]{2,1,0:T(8,128)(2,1)}), bf16[1,4096,512]{2,1,0:T(8,128)(2,1)}) %all-gather.24.cloned.1.call-update) | async-done | bytes 4194320 | tf_op jit(solution)/shard_map/all_gather | solution.py:120
  127.1 4.1 fusion.16
  131.4 0.3 fusion.96
  132.0 144.8 %all-gather.26.cloned.1.call-done = bf16[1,4096,1024]{2,1,0:T(8,128)(2,1)} async-done(((bf16[1,1024,1024]{2,1,0:T(8,128)(2,1)}), bf16[1,4096,1024]{2,1,0:T(8,128)(2,1)}) %all-gather.26.cloned.1.call-update) | async-done | bytes 8388624 | tf_op jit(solution)/shard_map/all_gather | solution.py:115
  276.8 5.5 fusion.35
  282.6 1.3 collective-permute-start.4
  283.9 1.3 collective-permute-start.7
  285.2 1.3 collective-permute-start.1
  286.5 0.3 fusion.97
  286.9 8.8 %collective-permute-done.4 = bf16[32,8,128]{2,1,0:T(8,128)(2,1)S(1)} collective-permute-done((bf16[32,8,128]{2,1,0:T(8,128)(2,1)S(1)}, bf16[32,8,128]{2,1,0:T(8,128)(2,1)S(1)}, u32[]{:S(2)}, u32[]{:S(2)}) %collective-permute-start.4) | collective-permute-done | bytes 65568 | tf_op jit(solution)/shard_map/ppermute | solution.py:21
  295.7 0.3 fusion.99
  296.0 0.3 fusion.100
  296.3 0.3 select_reduce_fusion.2
  296.6 1.3 collective-permute-start.8
  298.0 1.3 collective-permute-start.5
  299.3 0.3 fusion.98
  299.8 3.8 collective-permute-start.2
  303.9 1.2 collective-permute-done.2
  305.1 1.3 collective-permute-start.9
  306.4 54.3 %all-gather.22.cloned.1.call-done = bf16[1,4096,512]{2,1,0:T(8,128)(2,1)} async-done(((bf16[1,1024,512]{2,1,0:T(8,128)(2,1)}), bf16[1,4096,512]{2,1,0:T(8,128)(2,1)}) %all-gather.22.cloned.1.call-update) | async-done | bytes 4194320 | tf_op jit(solution)/shard_map/all_gather | solution.py:125
  360.7 4.2 fusion.21
  364.9 1.0 convert_element_type.54
  365.9 1.3 collective-permute-start.11
  367.2 1.3 collective-permute-start.13
  368.6 0.3 convolution_bitcast_fusion.2
  368.8 1.3 collective-permute-start.10
  370.2 2.2 collective-permute-done.11
  372.4 0.3 convolution_bitcast_fusion.1
  372.7 5.3 collective-permute-start.12
  378.0 0.3 convolution_bitcast_fusion
  378.3 1.3 collective-permute-start.14
  379.6 5.0 collective-permute-done.12
  384.6 5.1 collective-permute-done.14
  389.8 0.3 fusion.38
  390.1 124.0 %all-gather.28.cloned.1.call-done = bf16[1,1024,4096]{2,1,0:T(8,128)(2,1)} async-done(((bf16[1,1024,1024]{2,1,0:T(8,128)(2,1)}), bf16[1,1024,4096]{2,1,0:T(8,128)(2,1)}) %all-gather.28.cloned.1.call-update) | async-done | bytes 8388624 | tf_op jit(solution)/shard_map/all_gather | solution.py:171
  514.1 5.8 fusion.7
  520.0 34.4 %all-reduce.3.cloned.1.call-done = f32[32,4096]{1,0:T(8,128)} async-done(((f32[32,4096]{1,0:T(8,128)}), f32[32,4096]{1,0:T(8,128)}) %all-reduce.3.cloned.1.call-update) | async-done | bytes 524304 | tf_op jit(solution)/shard_map/psum | solution.py:174
  554.4 1.6 multiply_reduce_fusion
  556.1 0.8 multiply_convert_fusion
  556.9 0.6 dynamic-slice
  558.4 8.3 %all-reduce = s32[128]{0:T(128)S(1)} all-reduce(s32[128]{0:T(128)S(1)} %dynamic-update-slice), channel_id=1, replica_groups=mesh['groups'=2,'seq'=4,'tp'=2,'ref'=2] {'seq'}, use_global_device_ids=true, to_apply=%add | all-reduce | flops 128 | bytes 1024
  566.7 18.4 %all-gather.18.cloned.1.call-done = bf16[128,4096]{1,0:T(8,128)(2,1)} async-done(((bf16[32,4096]{1,0:T(8,128)(2,1)}), bf16[128,4096]{1,0:T(8,128)(2,1)}) %all-gather.18.cloned.1.call-update) | async-done | bytes 1048592 | tf_op jit(solution)/shard_map/all_gather | solution.py:177
  585.1 3.3 fusion.101
  588.6 19.0 %all-gather.10 = f32[8,1,128]{2,1,0:T(1,128)S(1)} all-gather(f32[1,1,128]{2,1,0:T(1,128)S(1)} %bitcast.284), channel_id=9, replica_groups=mesh['groups'=2,'seq'=4,'tp'=2,'ref'=2] {'seq','tp'}, dimensions={0}, use_global_device_ids=true | all-gather | bytes 4608 | tf_op jit(solution)/shard_map/all_gather | solution.py:25
  607.6 16.3 %all-gather.9 = f32[8,1,128]{2,1,0:T(1,128)S(1)} all-gather(f32[1,1,128]{2,1,0:T(1,128)S(1)} %bitcast.283), channel_id=8, replica_groups=mesh['groups'=2,'seq'=4,'tp'=2,'ref'=2] {'seq','tp'}, dimensions={0}, use_global_device_ids=true | all-gather | bytes 4608 | tf_op jit(solution)/shard_map/all_gather | solution.py:25
  623.8 18.3 %all-gather.8 = f32[8,1,128]{2,1,0:T(1,128)S(1)} all-gather(f32[1,1,128]{2,1,0:T(1,128)S(1)} %bitcast.280), channel_id=7, replica_groups=mesh['groups'=2,'seq'=4,'tp'=2,'ref'=2] {'seq','tp'}, dimensions={0}, use_global_device_ids=true | all-gather | bytes 4608 | tf_op jit(solution)/shard_map/all_gather | solution.py:25
  642.1 0.3 while.19
  642.5 0.7 select_reduce_fusion.5
  (93 shorter events, 3.4 us)
Async XLA Ops:
  6.5 3.5 copy-start.3
  6.5 13.5 %copy-start.4 = (s32[256]{0:T(256)S(1)}, s32[256]{0:T(256)}, u32[]{:S(2)}) copy-start(s32[256]{0:T(256)} %param.16) | copy-start | bytes 3076
  6.5 14.2 %copy-start.5 = (s32[256]{0:T(256)S(1)}, s32[256]{0:T(256)}, u32[]{:S(2)}) copy-start(s32[256]{0:T(256)} %param.15) | copy-start | bytes 3076
  6.5 38.2 %all-gather.20.cloned.1.call-start = ((), (), s32[]{:S(2)}) async-start(), calls=%async_computation.2 | async-start | bytes 3145728 | tf_op jit(solution)/shard_map/all_gather | solution.py:87
  7.3 119.8 %copy-start.1 = (f32[1,4096]{1,0:T(1,128)S(1)}, f32[1,4096]{1,0:T(1,128)}, u32[]{:S(2)}) copy-start(f32[1,4096]{1,0:T(1,128)} %param.17) | copy-start | bytes 49156
  7.3 119.8 %all-gather.24.cloned.1.call-start = ((), (), s32[]{:S(2)}) async-start(), calls=%async_computation.4 | async-start | bytes 5242880 | tf_op jit(solution)/shard_map/all_gather | solution.py:120
  8.0 268.8 %all-gather.26.cloned.1.call-start = ((), (), s32[]{:S(2)}) async-start(), calls=%async_computation.5 | async-start | bytes 10485760 | tf_op jit(solution)/shard_map/all_gather | solution.py:115
  8.8 352.0 %all-gather.22.cloned.1.call-start = ((), (), s32[]{:S(2)}) async-start(), calls=%async_computation.3 | async-start | bytes 5242880 | tf_op jit(solution)/shard_map/all_gather | solution.py:125
  9.3 504.8 %all-gather.28.cloned.1.call-start = ((), (), s32[]{:S(2)}) async-start(), calls=%async_computation.6 | async-start | bytes 10485760 | tf_op jit(solution)/shard_map/all_gather | solution.py:171
  9.9 544.5 %all-reduce.3.cloned.1.call-start = ((), (), s32[]{:S(2)}) async-start(), calls=%async_computation | async-start | bytes 1048576 | tf_op jit(solution)/shard_map/psum | solution.py:174
  20.9 5.5 collective-permute-start
  22.2 6.5 collective-permute-start.3
  23.5 8.4 %collective-permute-start.6 = (s32[2,32]{1,0:T(2,128)S(1)}, s32[2,32]{1,0:T(2,128)S(1)}, u32[]{:S(2)}, u32[]{:S(2)}) collective-permute-start(s32[2,32]{1,0:T(2,128)S(1)} %pad_add_fusion), channel_id=1, source_target_pairs={{12,0},{13,1},{14,2},{15,3},{28,16},{29,17},{30,18},{31,19}} | collective-permute-start | bytes 776 | tf_op jit(solution)/shard_map/ppermute | solution.py:21
  131.2 145.6 %copy-start = (bf16[1,256,4096]{2,1,0:T(8,128)(2,1)S(1)}, bf16[1,256,4096]{2,1,0:T(8,128)(2,1)}, u32[]{:S(2)}) copy-start(bf16[1,256,4096]{2,1,0:T(8,128)(2,1)} %all-gather.20.cloned.1.call-done) | copy-start | bytes 6291460
  282.6 13.0 %collective-permute-start.4 = (bf16[32,8,128]{2,1,0:T(8,128)(2,1)S(1)}, bf16[32,8,128]{2,1,0:T(8,128)(2,1)S(1)}, u32[]{:S(2)}, u32[]{:S(2)}) collective-permute-start(bf16[32,8,128]{2,1,0:T(8,128)(2,1)S(1)} %pad_maximum_fusion), channel_id=1, source_target_pairs={{8,0},{12,4},{9,1},{13,5},{10,2},{14,6},{11,3},{15,7},{24,16},{28,... | collective-permute-start | bytes 196616 | tf_op jit(solution)/shard_map/ppermute | solution.py:21
  283.9 11.8 %collective-permute-start.7 = (bf16[32,8,128]{2,1,0:T(8,128)(2,1)S(1)}, bf16[32,8,128]{2,1,0:T(8,128)(2,1)S(1)}, u32[]{:S(2)}, u32[]{:S(2)}) collective-permute-start(bf16[32,8,128]{2,1,0:T(8,128)(2,1)S(1)} %pad_maximum_fusion), channel_id=1, source_target_pairs={{12,0},{13,1},{14,2},{15,3},{28,16},{29,17},{30,18},{31,19}} | collective-permute-start | bytes 196616 | tf_op jit(solution)/shard_map/ppermute | solution.py:21
  285.2 14.0 %collective-permute-start.1 = (bf16[32,8,128]{2,1,0:T(8,128)(2,1)S(1)}, bf16[32,8,128]{2,1,0:T(8,128)(2,1)S(1)}, u32[]{:S(2)}, u32[]{:S(2)}) collective-permute-start(bf16[32,8,128]{2,1,0:T(8,128)(2,1)S(1)} %pad_maximum_fusion), channel_id=1, source_target_pairs={{4,0},{8,4},{12,8},{5,1},{9,5},{13,9},{6,2},{10,6},{14,10},{7,3},{... | collective-permute-start | bytes 196616 | tf_op jit(solution)/shard_map/ppermute | solution.py:21
  296.6 7.2 %collective-permute-start.8 = (f32[2,4,2,32]{3,2,1,0:T(2,128)S(1)}, f32[2,4,2,32]{3,2,1,0:T(2,128)S(1)}, u32[]{:S(2)}, u32[]{:S(2)}) collective-permute-start(f32[2,4,2,32]{3,2,1,0:T(2,128)S(1)} %pad_maximum_fusion.3), channel_id=1, source_target_pairs={{0,12},{1,13},{2,14},{3,15},{16,28},{17,29},{18,30},{19,31}} | collective-permute-start | bytes 6152 | tf_op jit(solution)/shard_map/ppermute | solution.py:21
  298.0 5.9 collective-permute-start.5
  299.8 5.3 collective-permute-start.2
  305.1 63.4 %collective-permute-start.9 = (f32[2,4,2,32]{3,2,1,0:T(2,128)S(1)}, f32[2,4,2,32]{3,2,1,0:T(2,128)S(1)}, u32[]{:S(2)}, u32[]{:S(2)}) collective-permute-start(f32[2,4,2,32]{3,2,1,0:T(2,128)S(1)} %pad_maximum_fusion.4), channel_id=1, source_target_pairs={{4,0},{8,4},{12,8},{5,1},{9,5},{13,9},{6,2},{10,6},{14,10},{7,3},{... | collective-permute-start | bytes 6152 | tf_op jit(solution)/shard_map/ppermute | solution.py:21
  365.9 6.4 collective-permute-start.11
  367.2 10.7 %collective-permute-start.13 = (f32[2,4,2,32]{3,2,1,0:T(2,128)S(1)}, f32[2,4,2,32]{3,2,1,0:T(2,128)S(1)}, u32[]{:S(2)}, u32[]{:S(2)}) collective-permute-start(f32[2,4,2,32]{3,2,1,0:T(2,128)S(1)} %pad_maximum_fusion.4), channel_id=1, source_target_pairs={{12,0},{13,1},{14,2},{15,3},{28,16},{29,17},{30,18},{31,19}} | collective-permute-start | bytes 6152 | tf_op jit(solution)/shard_map/ppermute | solution.py:21
  368.8 10.8 %collective-permute-start.10 = (f32[32,4,2,128]{3,0,2,1:T(8,128)S(1)}, f32[32,4,2,128]{3,0,2,1:T(8,128)S(1)}, u32[]{:S(2)}, u32[]{:S(2)}) collective-permute-start(f32[32,4,2,128]{3,0,2,1:T(8,128)S(1)} %convolution_bitcast_fusion.2), channel_id=1, source_target_pairs={{0,4},{4,8},{8,12},{1,5},{5,9},{9,13},{2,6},{6,10},{10,14},{3,7},{... | collective-permute-start | bytes 393224 | tf_op jit(solution)/shard_map/ppermute | solution.py:21
  372.7 12.0 %collective-permute-start.12 = (f32[32,4,2,128]{3,0,2,1:T(8,128)S(1)}, f32[32,4,2,128]{3,0,2,1:T(8,128)S(1)}, u32[]{:S(2)}, u32[]{:S(2)}) collective-permute-start(f32[32,4,2,128]{3,0,2,1:T(8,128)S(1)} %convolution_bitcast_fusion.1), channel_id=1, source_target_pairs={{0,8},{4,12},{1,9},{5,13},{2,10},{6,14},{3,11},{7,15},{16,24},{20,... | collective-permute-start | bytes 393224 | tf_op jit(solution)/shard_map/ppermute | solution.py:21
  378.3 11.5 %collective-permute-start.14 = (f32[32,4,2,128]{3,0,2,1:T(8,128)S(1)}, f32[32,4,2,128]{3,0,2,1:T(8,128)S(1)}, u32[]{:S(2)}, u32[]{:S(2)}) collective-permute-start(f32[32,4,2,128]{3,0,2,1:T(8,128)S(1)} %convolution_bitcast_fusion), channel_id=1, source_target_pairs={{0,12},{1,13},{2,14},{3,15},{16,28},{17,29},{18,30},{19,31}} | collective-permute-start | bytes 393224 | tf_op jit(solution)/shard_map/ppermute | solution.py:21
  390.1 165.9 %copy-start.2 = (f32[1,4096]{1,0:T(1,128)S(1)}, f32[1,4096]{1,0:T(1,128)}, u32[]{:S(2)}) copy-start(f32[1,4096]{1,0:T(1,128)} %param.18) | copy-start | bytes 49156
  519.9 37.0 %copy-start.6 = (u32[32]{0:T(128)S(1)}, u32[32]{0:T(128)}, u32[]{:S(2)}) copy-start(u32[32]{0:T(128)} %constant.122) | copy-start | bytes 388
  519.9 65.1 %all-gather.18.cloned.1.call-start = ((), (), s32[]{:S(2)}) async-start(), calls=%async_computation.1 | async-start | bytes 1310720 | tf_op jit(solution)/shard_map/all_gather | solution.py:177
Sparse Core Ops, SparseCore 0:
  8.9 35.8 all-gather.19
  46.3 80.7 all-gather.23
  128.6 148.1 all-gather.25
  278.2 82.4 all-gather.21
  362.2 151.9 all-gather.27
  520.1 34.3 all-reduce.2
  557.0 27.9 all-gather.17
where the time goes:
time: 651 us; the launch traced here: 650 us
  waiting for transfers between devices  501 us (77%)
  blocking collectives  71.7 us (11%)
  matrix products  26.8 us (4%)
  starting transfers between devices  26.2 us (4%)
  between operations  14.7 us (2%)
  other arithmetic  6.9 us (1%)
    all_gather x1, waiting for transfers between devices, shards(): lax.all_gather(w_query[0], 'seq', axis=0, tiled=True)  145 us
    all_gather x1, waiting for transfers between devices, shards(): lax.all_gather(w_out[0], 'seq', axis=1, tiled=True)  124 us
    all_gather x1, waiting for transfers between devices, shards(): lax.all_gather(w_key[0], 'seq', axis=0, tiled=True)  80.2 us
    all_gather x1, waiting for transfers between devices, shards(): lax.all_gather(w_value[0], 'seq', axis=0, tiled=True)  54.3 us
    all_gather x3, blocking collectives, joined(): gathered = jax.tree.map(lambda a: lax.all_gather(a, axis), part)  53.5 us
    psum x1, waiting for transfers between devices, shards(): summed = lax.psum(partial_out, 'tp')  34.4 us
    ppermute x15, waiting for transfers between devices, passed_along(): return lax.ppermute(value, axis, pairs)  28.8 us
    ppermute x15, starting transfers between devices, passed_along(): return lax.ppermute(value, axis, pairs)  25.9 us
  transfers between devices with their start and end apart: 22, of which 15 were waited for; matrix products, arithmetic and copies ran while one was open for 4% of the time, Pallas kernels for 0%

commit v1 on v0

--- a/solution.py
+++ b/solution.py
@@ -1,10 +1,13 @@
+import functools
+
 import jax
 import jax.numpy as jnp
 from jax import lax
+from jax.experimental import pallas as pl
+from jax.experimental.pallas import tpu as pltpu
 from jax.sharding import PartitionSpec as P
 
 HEAD_DIM = 128
-VOCAB_DEV = 512
 WINDOW = 2048
 CAP = 32
 SEGMENTS = 4
@@ -67,7 +70,7 @@
     return jnp.einsum("ngck,knd->cngd", weights, value_block, preferred_element_type=jnp.float32)
 
 
-def shards(
+def gathered_weights(
     hidden,
     segment_ids,
     targets,
@@ -177,10 +180,10 @@
     all_rows = lax.all_gather(final, "seq", axis=0, tiled=True)
     all_targets = lax.all_gather(row_target, "seq", axis=0, tiled=True)
     logits = jnp.dot(all_rows, head[0], preferred_element_type=jnp.float32)
-    vocab_start = (seq_index * lax.axis_size("tp") + lax.axis_index("tp")) * VOCAB_DEV
+    vocab_start = (seq_index * lax.axis_size("tp") + lax.axis_index("tp")) * head.shape[2]
     local_top = jnp.max(logits, axis=1)
     local_total = jnp.sum(jnp.exp(logits - local_top[:, None]), axis=1)
-    hit = all_targets[:, None] == vocab_start + jnp.arange(VOCAB_DEV, dtype=jnp.int32)[None, :]
+    hit = all_targets[:, None] == vocab_start + jnp.arange(head.shape[2], dtype=jnp.int32)[None, :]
     local_target = jnp.sum(jnp.where(hit, logits, 0.0), axis=1)
     merged_top, merged_total, merged_target = joined(
         (local_top, local_total, local_target), ("seq", "tp"), combine_stats
@@ -188,6 +191,377 @@
     logp = merged_target - (merged_top + jnp.log(merged_total))
     own = lax.dynamic_slice_in_dim(logp, seq_index * CAP, CAP, 0)
     placed = jnp.sum(jnp.where(picks, own[:, None], 0.0), axis=0)
+    return placed[None, :].astype(jnp.float32)
+
+
+def place():
+    return lax.axis_index("seq"), lax.axis_index("tp")
+
+
+def greet(peers):
+    barrier = pltpu.get_barrier_semaphore()
+    for peer in peers:
+        pl.semaphore_signal(barrier, inc=1, device_id=peer, device_id_type=pl.DeviceIdType.MESH)
+    pl.semaphore_wait(barrier, len(peers))
+
+
+def remote(source, target, send, recv, peer):
+    return pltpu.make_async_remote_copy(
+        src_ref=source,
+        dst_ref=target,
+        send_sem=send,
+        recv_sem=recv,
+        device_id=peer,
+        device_id_type=pl.DeviceIdType.MESH,
+    )
+
+
+def everyone(seq, tp):
+    s, t = place()
+    return [
+        ((d, e), {"seq": lax.rem(s + d, seq), "tp": lax.rem(t + e, tp)})
+        for d in range(seq)
+        for e in range(tp)
+        if (d, e) != (0, 0)
+    ]
+
+
+def tell_all(seq, tp, value, out, send, recv):
+    s, t = place()
+    out[s, t] = value[...]
+    copies = []
+    for number, (_, peer) in enumerate(everyone(seq, tp)):
+        copy = remote(value, out.at[s, t], send.at[number], recv.at[number], peer)
+        copy.start()
+        copies.append(copy)
+    return copies
+
+
+def spread_kernel(seq, big, meta, out, told, half, send, recv, fsend, frecv, msend, mrecv, xsend, xrecv):
+    s, t = place()
+    other = 1 - t
+    width = out.shape[-1]
+    per = seq // 2
+    greet([peer for _, peer in everyone(seq, 2)])
+    beside = {"seq": s, "tp": other}
+    first = remote(big.at[other], half, xsend, xrecv, beside)
+    first.start()
+    messages = tell_all(seq, 2, meta, told, msend, mrecv)
+
+    def blocks(base, view):
+        for i in range(per):
+            target = base * per + i
+
+            @pl.when(target != s)
+            def _():
+                remote(
+                    view(i), out.at[s, t], send.at[base * per + i], recv.at[s], {"seq": target, "tp": t}
+                ).start()
+
+            @pl.when(target == s)
+            def _():
+                remote(view(i), out.at[s, t], fsend.at[s], frecv.at[s], beside).start()
+                out[s, t] = view(i)[...]
+
+    own = lambda i: big.at[t, :, pl.ds(i * width, width)]
+    got = lambda i: half.at[:, pl.ds(i * width, width)]
+    blocks(t, own)
+    first.wait_recv()
+    blocks(other, got)
+    for d in (1, seq - 1, *range(2, seq - 1)):
+        source = lax.rem(s + d, seq)
+        remote(out.at[source, t], out.at[source, t], send.at[source], recv.at[source], beside).wait_recv()
+        remote(out.at[source, t], out.at[source, t], fsend.at[source], frecv.at[source], beside).start()
+    first.wait_send()
+    for d in range(seq):
+        source = lax.rem(s + d, seq)
+        if d:
+            remote(own(0), out.at[s, t], send.at[source], recv.at[source], beside).wait_send()
+        remote(out.at[source, t], out.at[source, other], fsend.at[source], frecv.at[source], beside).wait()
+    for copy in messages:
+        copy.wait()
+
+
+def spread(big, meta, seq, width):
+    rows = big.shape[1]
+    return pl.pallas_call(
+        functools.partial(spread_kernel, seq),
+        out_shape=(
+            jax.ShapeDtypeStruct((seq, 2, rows, width), jnp.bfloat16),
+            jax.ShapeDtypeStruct((seq, 2) + meta.shape, jnp.float32),
+        ),
+        in_specs=[pl.BlockSpec(memory_space=pltpu.VMEM)] * 2,
+        out_specs=[pl.BlockSpec(memory_space=pltpu.VMEM)] * 2,
+        scratch_shapes=[pltpu.VMEM(big.shape[1:], jnp.bfloat16)]
+        + [pltpu.SemaphoreType.DMA((seq,))] * 4
+        + [pltpu.SemaphoreType.DMA((2 * seq,))] * 2
+        + [pltpu.SemaphoreType.DMA] * 2,
+        compiler_params=pltpu.CompilerParams(collective_id=0, has_side_effects=True),
+    )(big, meta)
+
+
+def scatter_kernel(seq, count, *refs):
+    parts, outs, (send, recv) = refs[:count], refs[count : 2 * count], refs[2 * count :]
+    s, t = place()
+    greet([{"seq": lax.rem(s + d, seq), "tp": t} for d in range(1, seq)])
+    copies = []
+    for d in (2, *range(1, 2), *range(3, seq)):
+        target = lax.rem(s + d, seq)
+        for number, (part, out) in enumerate(zip(parts, outs)):
+            width = out.shape[-1]
+            columns = pl.ds(pl.multiple_of(target * width, width), width)
+            copy = remote(
+                part.at[:, columns],
+                out.at[d],
+                send.at[d, number],
+                recv.at[d, number],
+                {"seq": target, "tp": t},
+            )
+            copy.start()
+            copies.append(copy)
+    for part, out in zip(parts, outs):
+        width = out.shape[-1]
+        out[0] = part[:, pl.ds(pl.multiple_of(s * width, width), width)]
+    for copy in copies:
+        copy.wait()
+
+
+def scatter(parts, seq):
+    count = len(parts)
+    return pl.pallas_call(
+        functools.partial(scatter_kernel, seq, count),
+        out_shape=tuple(
+            jax.ShapeDtypeStruct((seq, p.shape[0], p.shape[1] // seq), p.dtype) for p in parts
+        ),
+        in_specs=[pl.BlockSpec(memory_space=pltpu.VMEM)] * count,
+        out_specs=[pl.BlockSpec(memory_space=pltpu.VMEM)] * count,
+        scratch_shapes=[pltpu.SemaphoreType.DMA((seq, count))] * 2,
+        compiler_params=pltpu.CompilerParams(collective_id=1, has_side_effects=True),
+    )(*parts)
+
+
+def heads_kernel(seq, part, out, send, recv):
+    s, t = place()
+    width = part.shape[1]
+    greet([{"seq": lax.rem(s + d, seq), "tp": t} for d in range(1, seq)])
+    mine = pl.ds(pl.multiple_of(s * width, width), width)
+    copies = []
+    for d in range(1, seq):
+        copy = remote(
+            part, out.at[:, mine], send.at[d], recv.at[d], {"seq": lax.rem(s + d, seq), "tp": t}
+        )
+        copy.start()
+        copies.append(copy)
+    out[:, mine] = part[...]
+    for copy in copies:
+        copy.wait()
+
+
+def gather_heads(part, seq):
+    return pl.pallas_call(
+        functools.partial(heads_kernel, seq),
+        out_shape=jax.ShapeDtypeStruct((part.shape[0], part.shape[1] * seq), part.dtype),
+        in_specs=[pl.BlockSpec(memory_space=pltpu.VMEM)],
+        out_specs=pl.BlockSpec(memory_space=pltpu.VMEM),
+        scratch_shapes=[pltpu.SemaphoreType.DMA((seq,))] * 2,
+        compiler_params=pltpu.CompilerParams(collective_id=2, has_side_effects=True),
+    )(part)
+
+
+def rows_kernel(seq, part, squares, out, told, send, recv, fsend, frecv, msend, mrecv):
+    s, t = place()
+    rows, width = part.shape
+    greet([peer for _, peer in everyone(seq, 2)])
+    beside = {"seq": s, "tp": 1 - t}
+
+    def spot(source, half):
+        return out.at[
+            pl.ds(pl.multiple_of(half * rows, rows), rows),
+            pl.ds(pl.multiple_of(source * width, width), width),
+        ]
+
+    copies = []
+    for d in (2, 1, 3)[: seq - 1]:
+        copy = remote(part, spot(s, t), send.at[d], recv.at[d], {"seq": lax.rem(s + d, seq), "tp": t})
+        copy.start()
+        copies.append((d, copy))
+    aside = remote(part, spot(s, t), fsend.at[0], frecv.at[0], beside)
+    aside.start()
+    forwards = [aside]
+    messages = tell_all(seq, 2, squares, told, msend, mrecv)
+    spot(s, t)[...] = part[...]
+    for d, copy in copies[1:] + copies[:1]:
+        copy.wait_recv()
+        source = lax.rem(s - d + seq, seq)
+        forward = remote(spot(source, t), spot(source, t), fsend.at[d], frecv.at[d], beside)
+        forward.start()
+        forwards.append(forward)
+    for _, copy in copies:
+        copy.wait_send()
+    for copy in forwards + messages:
+        copy.wait()
+
+
+def gather_rows(part, squares, seq):
+    rows, width = part.shape
+    return pl.pallas_call(
+        functools.partial(rows_kernel, seq),
+        out_shape=(
+            jax.ShapeDtypeStruct((2 * rows, width * seq), part.dtype),
+            jax.ShapeDtypeStruct((seq, 2) + squares.shape, jnp.float32),
+        ),
+        in_specs=[pl.BlockSpec(memory_space=pltpu.VMEM)] * 2,
+        out_specs=[pl.BlockSpec(memory_space=pltpu.VMEM)] * 2,
+        scratch_shapes=[pltpu.SemaphoreType.DMA((seq,))] * 4
+        + [pltpu.SemaphoreType.DMA((2 * seq,))] * 2,
+        compiler_params=pltpu.CompilerParams(collective_id=3, has_side_effects=True),
+    )(part, squares)
+
+
+def stats_kernel(seq, stats, told, send, recv):
+    greet([peer for _, peer in everyone(seq, 2)])
+    for copy in tell_all(seq, 2, stats, told, send, recv):
+        copy.wait()
+
+
+def gather_stats(stats, seq):
+    return pl.pallas_call(
+        functools.partial(stats_kernel, seq),
+        out_shape=jax.ShapeDtypeStruct((seq, 2) + stats.shape, jnp.float32),
+        in_specs=[pl.BlockSpec(memory_space=pltpu.VMEM)],
+        out_specs=pl.BlockSpec(memory_space=pltpu.VMEM),
+        scratch_shapes=[pltpu.SemaphoreType.DMA((2 * seq,))] * 2,
+        compiler_params=pltpu.CompilerParams(collective_id=4, has_side_effects=True),
+    )(stats)
+
+
+def padded(rows, lanes):
+    stacked = jnp.stack([r.astype(jnp.float32) for r in rows])
+    return jnp.pad(stacked, ((0, 8 - len(rows)), (0, lanes - stacked.shape[1])))
+
+
+def picks_of(mask):
+    ranking = jnp.cumsum(mask, axis=-1) - 1
+    return (mask[..., None, :] == 1) & (
+        ranking[..., None, :] == jnp.arange(CAP, dtype=jnp.int32)[:, None]
+    )
+
+
+def moved_rows(
+    hidden,
+    segment_ids,
+    targets,
+    loss_mask,
+    attn_gain,
+    final_gain,
+    w_query,
+    w_key,
+    w_value,
+    w_out,
+    head,
+):
+    seq = lax.axis_size("seq")
+    s, t = place()
+    tokens, features = hidden.shape[1:]
+    model = features * 2
+    width = w_key.shape[1]
+    length = seq * tokens
+    x = hidden[0]
+    xfloat = x.astype(jnp.float32)
+    gain = lax.dynamic_slice_in_dim(attn_gain[0], t * features, features)
+    scaled = (xfloat * gain).astype(jnp.bfloat16)
+    squares = jnp.sum(xfloat * xfloat, axis=1)
+    chooser = picks_of(loss_mask).astype(jnp.bfloat16)
+    pick_scaled = jnp.dot(chooser, scaled, preferred_element_type=jnp.float32).astype(jnp.bfloat16)
+    pick_raw = jnp.dot(chooser, x, preferred_element_type=jnp.float32).astype(jnp.bfloat16)
+    big = jnp.concatenate(
+        [
+            scaled.reshape(2, tokens // 2, features),
+            pick_scaled.reshape(2, CAP // 2, features),
+            pick_raw.reshape(2, CAP // 2, features),
+        ],
+        axis=1,
+    )
+    meta = padded([segment_ids, loss_mask, targets, squares], tokens)
+    spread_out, told = spread(big, meta, seq, width)
+
+    half = tokens // 2
+    token_block = spread_out[:, :, :half].reshape(length, width)
+    row_block = spread_out[:, :, half : half + CAP // 2].reshape(seq * CAP, width)
+    raw_block = spread_out[:, :, half + CAP // 2 :].reshape(seq * CAP, width)
+    key_part = jnp.dot(token_block, w_key[0], preferred_element_type=jnp.float32)
+    value_part = jnp.dot(token_block, w_value[0], preferred_element_type=jnp.float32)
+    query_part = jnp.dot(row_block, w_query[0], preferred_element_type=jnp.float32)
+
+    keys, values, query = scatter(
+        [p.astype(jnp.bfloat16) for p in (key_part, value_part, query_part)], seq
+    )
+
+    whole = told[:, 0].astype(jnp.int32)
+    segments = whole[:, 0].reshape(length)
+    masks = whole[:, 1]
+    position = jnp.arange(length, dtype=jnp.int32)
+    member = segments[None, :] == jnp.arange(SEGMENTS, dtype=jnp.int32)[:, None]
+    starts = jnp.min(jnp.where(member, position[None, :], FARTHEST), axis=1)
+    token_start = jnp.sum(jnp.where(member, starts[:, None], 0), axis=0)
+    offsets = position - token_start
+    scale = lax.rsqrt((told[:, 0, 3] + told[:, 1, 3]) / model + EPS)
+    picks = picks_of(masks)
+
+    def chosen(values):
+        return jnp.sum(jnp.where(picks, values.reshape(seq, 1, tokens), 0), axis=2).reshape(-1)
+
+    row_pos = chosen(position)
+    row_start = chosen(token_start)
+    row_target = chosen(whole[:, 2])
+    row_scale = chosen(scale)
+
+    def total(parts):
+        return jnp.sum(parts.astype(jnp.float32), axis=0)
+
+    key_all = total(keys) * scale.reshape(length, 1)
+    value_all = (total(values) * scale.reshape(length, 1)).astype(jnp.bfloat16)
+    query_all = total(query) * row_scale[:, None]
+    group = query_all.shape[1] // HEAD_DIM
+    key_all = rotate(key_all[:, None, :], offsets)[:, 0].astype(jnp.bfloat16)
+    query_all = rotate(query_all.reshape(seq * CAP, group, HEAD_DIM), row_pos - row_start).astype(
+        jnp.bfloat16
+    )
+    allowed = (position[None, :] <= row_pos[:, None]) & (position[None, :] >= row_start[:, None])
+    allowed = allowed & (row_pos[:, None] - position[None, :] < WINDOW)
+    scores = jnp.einsum("cgd,kd->gck", query_all, key_all, preferred_element_type=jnp.float32)
+    scores = jnp.where(allowed[None], scores * HEAD_DIM ** (-0.5), -1e30)
+    peak = jnp.max(scores, axis=-1, keepdims=True)
+    lifted = jnp.exp(scores - peak)
+    weights = (lifted / jnp.sum(lifted, axis=-1, keepdims=True)).astype(jnp.bfloat16)
+    attended = jnp.einsum("gck,kd->cgd", weights, value_all, preferred_element_type=jnp.float32)
+    attended = attended.astype(jnp.bfloat16).reshape(seq * CAP, group * HEAD_DIM)
+    attended = gather_heads(attended, seq)
+    partial_out = jnp.dot(attended, w_out[0], preferred_element_type=jnp.float32)
+
+    rows = seq * CAP // 2
+    away = lax.dynamic_slice_in_dim(partial_out, (1 - t) * rows, rows).astype(jnp.bfloat16)
+    here = lax.dynamic_slice_in_dim(partial_out, t * rows, rows)
+    here = here + lax.dynamic_slice_in_dim(raw_block, t * rows, rows).astype(jnp.float32)
+    state = here + lax.ppermute(away, "tp", [(0, 1), (1, 0)]).astype(jnp.float32)
+    late_gain = lax.dynamic_slice_in_dim(final_gain[0], s * width, width)
+    late = (state * late_gain).astype(jnp.bfloat16)
+    final, late_squares = gather_rows(late, padded([jnp.sum(state * state, axis=1)], 128), seq)
+    late_mean = jnp.sum(late_squares[:, :, 0, :rows], axis=0).reshape(-1) / model
+    logits = jnp.dot(final, head[0], preferred_element_type=jnp.float32)
+    logits = logits * lax.rsqrt(late_mean + EPS)[:, None]
+    entries = head.shape[2]
+    first_entry = (s * 2 + t) * entries
+    top = jnp.max(logits, axis=1)
+    exps = jnp.sum(jnp.exp(logits - top[:, None]), axis=1)
+    hit = row_target[:, None] == first_entry + jnp.arange(entries, dtype=jnp.int32)[None, :]
+    found = jnp.sum(jnp.where(hit, logits, 0.0), axis=1)
+    stats = gather_stats(padded([top, exps, found], seq * CAP), seq)
+    mine = lax.dynamic_slice_in_dim(stats.reshape(seq * 2, 8, seq * CAP), s * CAP, CAP, 2)
+    best = jnp.max(mine[:, 0], axis=0)
+    summed = jnp.sum(mine[:, 1] * jnp.exp(mine[:, 0] - best[None, :]), axis=0)
+    logp = jnp.sum(mine[:, 2], axis=0) - (best + jnp.log(summed))
+    placed = jnp.sum(jnp.where(picks_of(loss_mask), logp[:, None], 0.0), axis=0)
     return placed[None, :].astype(jnp.float32)
 
 
@@ -205,6 +579,13 @@
         P("ref", "tp", "seq"),
         P("ref", None, ("seq", "tp")),
     )
+
+    def shards(*args):
+        seq, tp = mesh.shape["seq"], mesh.shape["tp"]
+        own_heads = args[7].shape[2] // HEAD_DIM
+        moves = tp == 2 and seq == 4 and own_heads % seq == 0
+        return (moved_rows if moves else gathered_weights)(*args)
+
     return jax.shard_map(
         shards, mesh=mesh, in_specs=placed, out_specs=P("ref", ("groups", "seq")), check_vma=False
     )

time: 651 us -> 227 us (0.35)
  waiting for transfers between devices: 501 us -> 4.16 us
  Pallas kernels: 0 us -> 170 us
  blocking collectives: 71.7 us -> 0 us
  starting transfers between devices: 26.2 us -> 0.07 us
  other arithmetic: 6.9 us -> 23.7 us
  between operations: 14.7 us -> 0.35 us
  matrix products: 26.8 us -> 18.5 us
  local copies, waits for them, and re-layouts: 2.89 us -> 9.42 us
    all_gather x6 -> x0, waiting for transfers between devices: 434 us -> none  [the longest x1 145 us: shards(): lax.all_gather(w_query[0], 'seq', axis=0, tiled=True)]
    pallas_call x0 -> x5, Pallas kernels: none -> 170 us  [the longest x1 62.5 us: spread(): pl.pallas_call(functools.partial(spread_kernel, seq), out_shape=(jax.Shap...]
    all_gather x3 -> x0, blocking collectives: 53.5 us -> none  [joined(): gathered = jax.tree.map(lambda a: lax.all_gather(a, axis), part)]
    psum x1 -> x0, waiting for transfers between devices: 34.4 us -> none  [shards(): summed = lax.psum(partial_out, 'tp')]
    ppermute x15 -> x1, starting transfers between devices: 25.9 us -> 0.07 us  [moved_rows(): lax.ppermute(away, 'tp', [(0, 1), (1, 0)]).astype(jnp.float32)]
    ppermute x15 -> x1, waiting for transfers between devices: 28.8 us -> 4.16 us  [moved_rows(): lax.ppermute(away, 'tp', [(0, 1), (1, 0)]).astype(jnp.float32)]
    pmin x1 -> x0, blocking collectives: 9.95 us -> none  [shards(): starts = lax.pmin(local_first, 'seq')]
    dot_general x14 -> x9, matrix products: 26.8 us -> 17.8 us  [the longest x1 4.25 us: moved_rows(): jnp.dot(token_block, w_value[0], preferred_element_type=jnp.float32)]
  transfers between devices with their start and end apart: 22 -> 1, of which waited for: 15 -> 1; matrix products, arithmetic and copies ran while one was open for 4% -> 0% of each run, Pallas kernels for 0% -> 0%
where the time goes in v1:
time: 227 us; the launch traced here: 226 us
  Pallas kernels  170 us (75%)
  other arithmetic  23.7 us (10%)
  matrix products  18.5 us (8%)
  local copies, waits for them, and re-layouts  9.42 us (4%)
  waiting for transfers between devices  4.16 us (2%)
    pallas_call x1, Pallas kernels, spread(): pl.pallas_call(functools.partial(spread_kernel, seq), out_shape=(jax.Shap...  62.5 us
    pallas_call x1, Pallas kernels, scatter(): pl.pallas_call(functools.partial(scatter_kernel, seq, count), out_shape=t...  58.4 us
    pallas_call x1, Pallas kernels, gather_heads(): pl.pallas_call(functools.partial(heads_kernel, seq), out_shape=jax.ShapeD...  19.9 us
    pallas_call x1, Pallas kernels, gather_rows(): pl.pallas_call(functools.partial(rows_kernel, seq), out_shape=(jax.ShapeD...  18.8 us
    pallas_call x1, Pallas kernels, gather_stats(): pl.pallas_call(functools.partial(stats_kernel, seq), out_shape=jax.ShapeD...  9.95 us
  transfers between devices with their start and end apart: 1, of which 1 were waited for; matrix products, arithmetic and copies ran while one was open for 0% of the time, Pallas kernels for 0%

profile of v1, /device:TPU:0, one launch (start us, length us, event | category | flops | bytes accessed | tf_op | source)
XLA Modules:
  0.0 225.7 jit_solution(8804660862243093695)
XLA Ops:
  0.0 0.5 negate_power_fusion
  0.5 0.7 broadcast_compare_fusion.1
  1.2 0.7 convert_element_type.114
  1.9 1.0 reduce-window.15
  3.0 0.1 slice_reduce_fusion.1
  3.2 0.7 convert_element_type.113
  3.9 0.7 convert_element_type.115
  4.6 1.5 fusion.4
  6.1 0.7 constant_dynamic-slice_fusion.3
  6.8 1.5 convolution_convert_fusion
  8.3 0.3 convolution_convert_fusion.1
  8.6 0.2 fusion.5
  8.8 1.2 pad_maximum_fusion.big
  10.0 0.6 select_maximum_fusion.meta
  10.6 62.5 %shard_map.109 = (bf16[4,2,160,1024]{3,2,1,0:T(8,128)(2,1)}, f32[4,2,8,256]{3,2,1,0:T(8,128)}) custom-call(bf16[2,160,2048]{2,1,0:T(8,128)(2,1)} %pad_maximum_fusion.big, f32[8,256]{1,0:T(8,128)} %select_maximum_fusion.meta), custom_call_target="tpu_custom_call" | custom-call | tf_op jit(solution)/shard_map/pallas_call | solution.py:287
  73.1 0.8 add_rsqrt_fusion
  73.9 0.8 convert_bitcast_fusion
  74.7 0.1 select_reduce_fusion.7
  74.9 0.1 select_reduce_fusion.6
  75.0 1.2 reduce-window.19
  76.3 0.1 copy.48
  76.4 0.1 copy.49
  76.6 0.3 select_reduce_fusion.1
  76.9 0.1 ge.17
  77.1 0.6 subtract_convert_fusion.2
  77.7 0.2 fusion.27
  77.8 1.1 fusion.55
  78.9 3.1 %slice.67 = bf16[4,2,128,1024]{3,2,1,0:T(8,128)(2,1)} slice(bf16[4,2,160,1024]{3,2,1,0:T(8,128)(2,1)} %get-tuple-element.12), slice={[0:4], [0:2], [0:128], [0:1024]} | slice | bytes 4194304 | tf_op jit(solution)/shard_map/slice | solution.py:489
  82.0 0.1 select_reduce_fusion.2
  82.1 0.7 mul.212
  82.8 4.3 %convolution_convert_fusion.2.refs_1_ = bf16[1024,512]{1,0:T(8,128)(2,1)} fusion(bf16[1024,1024]{1,0:T(8,128)(2,1)} %bitcast.108, bf16[1,1024,512]{2,1,0:T(8,128)(2,1)} %param.19), kind=kOutput, calls=%fused_computation.18 | convolution fusion | flops 1074266112 | bytes 4194304 | tf_op jit(solution)/shard_map/dot_general | solution.py:493
  87.0 2.2 convolution_convert_fusion.3.refs_0_
  89.3 1.1 fusion.14.refs_2_
  90.4 58.4 %shard_map.110 = (bf16[4,1024,128]{2,1,0:T(8,128)(2,1)}, bf16[4,1024,128]{2,1,0:T(8,128)(2,1)}, bf16[4,128,256]{2,1,0:T(8,128)(2,1)}) custom-call(bf16[1024,512]{1,0:T(8,128)(2,1)} %convolution_convert_fusion.3.refs_0_, bf16[1024,512]{1,0:T(8,128)(2,1)} %convolution_convert_fusion.2.refs_1_, bf16[128,1024]{1,0:T(8,128)(2,1)} %fusion.14.refs_2_), custom_call_target="tpu_custom_call" | custom-call | tf_op jit(solution)/shard_map/pallas_call | solution.py:331
  148.8 2.8 %convert_reduce_fusion = (f32[1024,128]{1,0:T(8,128)S(1)}, f32[1024,128]{1,0:T(8,128)}) fusion(bf16[4,1024,128]{2,1,0:T(8,128)(2,1)} %get-tuple-element.15, bf16[4,1024,128]{2,1,0:T(8,128)(2,1)} %get-tuple-element.13), kind=kLoop, calls=%fused_computation.15 | loop fusion | flops 1835008 | bytes 3145728 | tf_op jit(solution)/shard_map/reduce_sum | solution.py:520
  151.5 0.2 copy.50
  151.7 1.0 convert_reduce_fusion.2
  152.7 0.1 copy.51
  152.8 0.1 copy.52
  152.9 1.0 multiply_cosine_fusion.1
  154.0 1.8 fusion.33
  155.8 0.8 broadcast_multiply_fusion
  156.6 0.1 subtract_convert_fusion
  156.8 0.6 copy-done.5
  157.4 0.7 fusion.57
  158.0 1.4 fusion.13
  159.4 1.5 convolution_convert_fusion.4
  161.0 0.7 copy.63.part
  161.7 19.9 %shard_map.111 = bf16[128,1024]{1,0:T(8,128)(2,1)} custom-call(bf16[128,256]{1,0:T(8,128)(2,1)} %copy.63.part), custom_call_target="tpu_custom_call" | custom-call | tf_op jit(solution)/shard_map/pallas_call | solution.py:361
  181.6 2.1 fusion.6
  183.8 0.1 eq.87
  183.9 0.7 constant_dynamic-slice_fusion.1
  184.6 4.2 %collective-permute-done = bf16[64,1024]{1,0:T(8,128)(2,1)S(1)} collective-permute-done((bf16[64,1024]{1,0:T(8,128)(2,1)S(1)}, bf16[64,1024]{1,0:T(8,128)(2,1)S(1)}, u32[]{:S(2)}, u32[]{:S(2)}) %collective-permute-start) | collective-permute-done | bytes 131104 | tf_op jit(solution)/shard_map/ppermute | solution.py:546
  188.8 0.8 multiply_reduce_fusion
  189.6 0.6 pad.13.squares
  190.2 18.8 %shard_map.112 = (bf16[128,4096]{1,0:T(8,128)(2,1)}, f32[4,2,8,128]{3,2,1,0:T(8,128)}) custom-call(bf16[64,1024]{1,0:T(8,128)(2,1)} %get-tuple-element.27.part, f32[8,128]{1,0:T(8,128)} %pad.13.squares), custom_call_target="tpu_custom_call" | custom-call | tf_op jit(solution)/shard_map/pallas_call | solution.py:407
  209.1 0.8 slice_reduce_fusion
  209.8 0.1 rsqrt.31
  209.9 3.3 %fusion.58 = (f32[128]{0:T(128)S(1)}, f32[128,512]{1,0:T(8,128)S(1)}) fusion(f32[128]{0:T(128)S(1)} %rsqrt.31, bf16[128,4096]{1,0:T(8,128)(2,1)} %get-tuple-element.17, bf16[1,4096,512]{2,1,0:T(8,128)(2,1)} %param.21), kind=kOutput, calls=%fused_computation.125 | convolution fusion | flops 537001856 | bytes 5506048 | tf_op jit(solution)/shard_map/dot_general | solution.py:551
  213.2 0.2 exponential_reduce_fusion
  213.5 0.6 select_maximum_fusion.3.stats
  214.1 10.0 %shard_map.113 = f32[4,2,8,128]{3,2,1,0:T(8,128)} custom-call(f32[8,128]{1,0:T(8,128)} %select_maximum_fusion.3.stats), custom_call_target="tpu_custom_call" | custom-call | tf_op jit(solution)/shard_map/pallas_call | solution.py:428
  224.0 1.0 constant_dynamic-slice_fusion
  225.1 0.7 select_reduce_fusion.5
  (44 shorter events, 0.8 us)
Async XLA Ops:
  0.0 89.3 %copy-start = (bf16[1,1024,1024]{2,1,0:T(8,128)(2,1)S(1)}, bf16[1,1024,1024]{2,1,0:T(8,128)(2,1)}, u32[]{:S(2)}) copy-start(bf16[1,1024,1024]{2,1,0:T(8,128)(2,1)} %param.17) | copy-start | bytes 6291460
  0.0 8.3 %copy-start.1 = (bf16[1,256,2048]{2,1,0:T(8,128)(2,1)S(1)}, bf16[1,256,2048]{2,1,0:T(8,128)(2,1)}, u32[]{:S(2)}) copy-start(bf16[1,256,2048]{2,1,0:T(8,128)(2,1)} %param.11) | copy-start | bytes 3145732
  1.2 7.6 %copy-start.7 = (pred[256]{0:T(512)(128)(4,1)}, pred[256]{0:T(512)(128)(4,1)S(1)}, u32[]{:S(2)}) copy-start(pred[256]{0:T(512)(128)(4,1)S(1)} %broadcast_compare_fusion.1) | copy-start | bytes 772
  82.8 4.3 %copy-start.2 = (bf16[4,2,128,1024]{3,2,1,0:T(8,128)(2,1)S(1)}, bf16[4,2,128,1024]{3,2,1,0:T(8,128)(2,1)}, u32[]{:S(2)}) copy-start(bf16[4,2,128,1024]{3,2,1,0:T(8,128)(2,1)} %slice.67) | copy-start | bytes 6291460
  82.8 4.3 %copy-start.9 = (bf16[1,1024,512]{2,1,0:T(8,128)(2,1)S(1)}, bf16[1,1024,512]{2,1,0:T(8,128)(2,1)}, u32[]{:S(2)}) copy-start(bf16[1,1024,512]{2,1,0:T(8,128)(2,1)} %param.18) | copy-start | bytes 3145732
  155.8 0.9 copy-start.3
  155.8 0.9 copy-start.4
  156.7 0.6 copy-start.5
  156.7 0.6 copy-start.6
  183.7 5.0 %collective-permute-start = (bf16[64,1024]{1,0:T(8,128)(2,1)S(1)}, bf16[64,1024]{1,0:T(8,128)(2,1)S(1)}, u32[]{:S(2)}, u32[]{:S(2)}) collective-permute-start(bf16[64,1024]{1,0:T(8,128)(2,1)S(1)} %dynamic-slice_convert_fusion), channel_id=1, source_target_pairs={{0,2},{2,0},{1,3},{3,1},{4,6},{6,4},{5,7},{7,5},{8,10},{10,8},{9,1... | collective-permute-start | bytes 393224 | tf_op jit(solution)/shard_map/ppermute | solution.py:546
  209.9 15.1 %copy-start.8 = (pred[256]{0:T(512)(128)(4,1)S(1)}, pred[256]{0:T(512)(128)(4,1)}, u32[]{:S(2)}) copy-start(pred[256]{0:T(512)(128)(4,1)} %copy-done.7) | copy-start | bytes 772

commit v2 on v1

--- a/solution.py
+++ b/solution.py
@@ -237,10 +237,35 @@
     return copies
 
 
-def spread_kernel(seq, big, meta, out, told, half, send, recv, fsend, frecv, msend, mrecv, xsend, xrecv):
+def project_kernel(
+    seq,
+    pick,
+    big,
+    meta,
+    w_query,
+    w_key,
+    w_value,
+    out,
+    raw,
+    told,
+    half,
+    blocks,
+    parts,
+    send,
+    recv,
+    fsend,
+    frecv,
+    msend,
+    mrecv,
+    psend,
+    precv,
+    xsend,
+    xrecv,
+):
     s, t = place()
     other = 1 - t
-    width = out.shape[-1]
+    width = blocks.shape[-1]
+    tokens = blocks.shape[2] - 2 * pick
     per = seq // 2
     greet([peer for _, peer in everyone(seq, 2)])
     beside = {"seq": s, "tp": other}
@@ -248,96 +273,137 @@
     first.start()
     messages = tell_all(seq, 2, meta, told, msend, mrecv)
 
-    def blocks(base, view):
+    def hand_out(base, view):
         for i in range(per):
             target = base * per + i
 
             @pl.when(target != s)
             def _():
                 remote(
-                    view(i), out.at[s, t], send.at[base * per + i], recv.at[s], {"seq": target, "tp": t}
+                    view(i),
+                    blocks.at[s, t],
+                    send.at[target],
+                    recv.at[s],
+                    {"seq": target, "tp": t},
                 ).start()
 
             @pl.when(target == s)
             def _():
-                remote(view(i), out.at[s, t], fsend.at[s], frecv.at[s], beside).start()
-                out[s, t] = view(i)[...]
+                remote(view(i), blocks.at[s, t], fsend.at[s], frecv.at[s], beside).start()
+                blocks[s, t] = view(i)[...]
 
     own = lambda i: big.at[t, :, pl.ds(i * width, width)]
     got = lambda i: half.at[:, pl.ds(i * width, width)]
-    blocks(t, own)
+    hand_out(t, own)
     first.wait_recv()
-    blocks(other, got)
-    for d in (1, seq - 1, *range(2, seq - 1)):
-        source = lax.rem(s + d, seq)
-        remote(out.at[source, t], out.at[source, t], send.at[source], recv.at[source], beside).wait_recv()
-        remote(out.at[source, t], out.at[source, t], fsend.at[source], frecv.at[source], beside).start()
+    hand_out(other, got)
+
+    def arrived(source):
+        return remote(
+            blocks.at[source, t], blocks.at[source, t], send.at[source], recv.at[source], beside
+        )
+
+    def passed(source):
+        return remote(
+            blocks.at[source, t], blocks.at[source, t], fsend.at[source], frecv.at[source], beside
+        )
+
+    def handed(chunk, d):
+        return remote(
+            parts.at[chunk, d],
+            out.at[d, chunk],
+            psend.at[chunk, d],
+            precv.at[chunk, d],
+            {"seq": lax.rem(s + d, seq), "tp": t},
+        )
+
+    def project(source, side):
+        chunk = source * 2 + side
+        rows = blocks[source, side, :tokens]
+        chosen = blocks[source, side, tokens : tokens + pick]
+        raw[source, side] = blocks[source, side, tokens + pick :]
+        dot = functools.partial(jnp.dot, preferred_element_type=jnp.float32)
+        for d in range(seq):
+            target = lax.rem(s + d, seq)
+            single = pl.ds(pl.multiple_of(target * HEAD_DIM, HEAD_DIM), HEAD_DIM)
+            wide = out.shape[-1]
+            double = pl.ds(pl.multiple_of(target * wide, wide), wide)
+            place_at = out.at[0, chunk] if d == 0 else parts.at[chunk, d]
+            place_at[:tokens, :HEAD_DIM] = dot(rows, w_key[:, single]).astype(jnp.bfloat16)
+            place_at[:tokens, HEAD_DIM:] = dot(rows, w_value[:, single]).astype(jnp.bfloat16)
+            place_at[tokens:] = dot(chosen, w_query[:, double]).astype(jnp.bfloat16)
+        for d in (2, 1, 3):
+            handed(chunk, d).start()
+
+    side_of = s // 2
+    partner = s + 1 - 2 * lax.rem(s, 2)
+
+    def step(number, carry):
+        source = jnp.where(
+            number == 0,
+            s,
+            jnp.where(
+                number == 1, partner, jnp.where(number == 2, 2 - side_of, 3 * (1 - side_of))
+            ),
+        )
+
+        @pl.when(number > 0)
+        def _():
+            arrived(source).wait_recv()
+            passed(source).start()
+
+        def both(side, more):
+            which = lax.rem(t + side, 2)
+
+            @pl.when(side == 1)
+            def _():
+                passed(source).wait_recv()
+
+            project(source, which)
+            return more
+
+        return lax.fori_loop(0, 2, both, carry)
+
+    lax.fori_loop(0, seq, step, 0)
     first.wait_send()
-    for d in range(seq):
-        source = lax.rem(s + d, seq)
-        if d:
-            remote(own(0), out.at[s, t], send.at[source], recv.at[source], beside).wait_send()
-        remote(out.at[source, t], out.at[source, other], fsend.at[source], frecv.at[source], beside).wait()
+    for source in range(seq):
+
+        @pl.when(source != s)
+        def _():
+            arrived(source).wait_send()
+
+        passed(source).wait_send()
     for copy in messages:
         copy.wait()
-
-
-def spread(big, meta, seq, width):
+    for d in range(1, seq):
+        for chunk in range(2 * seq):
+            handed(chunk, d).wait()
+
+
+def project(big, meta, w_query, w_key, w_value, seq, pick):
     rows = big.shape[1]
+    width = w_key.shape[0]
+    wide = w_query.shape[1] // seq
     return pl.pallas_call(
-        functools.partial(spread_kernel, seq),
+        functools.partial(project_kernel, seq, pick),
         out_shape=(
-            jax.ShapeDtypeStruct((seq, 2, rows, width), jnp.bfloat16),
+            jax.ShapeDtypeStruct((seq, 2 * seq, rows - pick, wide), jnp.bfloat16),
+            jax.ShapeDtypeStruct((seq, 2, pick, width), jnp.bfloat16),
             jax.ShapeDtypeStruct((seq, 2) + meta.shape, jnp.float32),
         ),
-        in_specs=[pl.BlockSpec(memory_space=pltpu.VMEM)] * 2,
-        out_specs=[pl.BlockSpec(memory_space=pltpu.VMEM)] * 2,
-        scratch_shapes=[pltpu.VMEM(big.shape[1:], jnp.bfloat16)]
+        in_specs=[pl.BlockSpec(memory_space=pltpu.VMEM)] * 5,
+        out_specs=[pl.BlockSpec(memory_space=pltpu.VMEM)] * 3,
+        scratch_shapes=[
+            pltpu.VMEM(big.shape[1:], jnp.bfloat16),
+            pltpu.VMEM((seq, 2, rows, width), jnp.bfloat16),
+            pltpu.VMEM((2 * seq, seq, rows - pick, wide), jnp.bfloat16),
+        ]
         + [pltpu.SemaphoreType.DMA((seq,))] * 4
         + [pltpu.SemaphoreType.DMA((2 * seq,))] * 2
+        + [pltpu.SemaphoreType.DMA((2 * seq, seq))] * 2
         + [pltpu.SemaphoreType.DMA] * 2,
         compiler_params=pltpu.CompilerParams(collective_id=0, has_side_effects=True),
-    )(big, meta)
-
-
-def scatter_kernel(seq, count, *refs):
-    parts, outs, (send, recv) = refs[:count], refs[count : 2 * count], refs[2 * count :]
-    s, t = place()
-    greet([{"seq": lax.rem(s + d, seq), "tp": t} for d in range(1, seq)])
-    copies = []
-    for d in (2, *range(1, 2), *range(3, seq)):
-        target = lax.rem(s + d, seq)
-        for number, (part, out) in enumerate(zip(parts, outs)):
-            width = out.shape[-1]
-            columns = pl.ds(pl.multiple_of(target * width, width), width)
-            copy = remote(
-                part.at[:, columns],
-                out.at[d],
-                send.at[d, number],
-                recv.at[d, number],
-                {"seq": target, "tp": t},
-            )
-            copy.start()
-            copies.append(copy)
-    for part, out in zip(parts, outs):
-        width = out.shape[-1]
-        out[0] = part[:, pl.ds(pl.multiple_of(s * width, width), width)]
-    for copy in copies:
-        copy.wait()
-
-
-def scatter(parts, seq):
-    count = len(parts)
-    return pl.pallas_call(
-        functools.partial(scatter_kernel, seq, count),
-        out_shape=tuple(
-            jax.ShapeDtypeStruct((seq, p.shape[0], p.shape[1] // seq), p.dtype) for p in parts
-        ),
-        in_specs=[pl.BlockSpec(memory_space=pltpu.VMEM)] * count,
-        out_specs=[pl.BlockSpec(memory_space=pltpu.VMEM)] * count,
-        scratch_shapes=[pltpu.SemaphoreType.DMA((seq, count))] * 2,
-        compiler_params=pltpu.CompilerParams(collective_id=1, has_side_effects=True),
-    )(*parts)
+    )(big, meta, w_query, w_key, w_value)
 
 
 def heads_kernel(seq, part, out, send, recv):
@@ -483,19 +549,9 @@
         axis=1,
     )
     meta = padded([segment_ids, loss_mask, targets, squares], tokens)
-    spread_out, told = spread(big, meta, seq, width)
-
+    parts, raw, told = project(big, meta, w_query[0], w_key[0], w_value[0], seq, CAP // 2)
     half = tokens // 2
-    token_block = spread_out[:, :, :half].reshape(length, width)
-    row_block = spread_out[:, :, half : half + CAP // 2].reshape(seq * CAP, width)
-    raw_block = spread_out[:, :, half + CAP // 2 :].reshape(seq * CAP, width)
-    key_part = jnp.dot(token_block, w_key[0], preferred_element_type=jnp.float32)
-    value_part = jnp.dot(token_block, w_value[0], preferred_element_type=jnp.float32)
-    query_part = jnp.dot(row_block, w_query[0], preferred_element_type=jnp.float32)
-
-    keys, values, query = scatter(
-        [p.astype(jnp.bfloat16) for p in (key_part, value_part, query_part)], seq
-    )
+    raw_block = raw.reshape(seq * CAP, width)
 
     whole = told[:, 0].astype(jnp.int32)
     segments = whole[:, 0].reshape(length)
@@ -516,12 +572,11 @@
     row_target = chosen(whole[:, 2])
     row_scale = chosen(scale)
 
-    def total(parts):
-        return jnp.sum(parts.astype(jnp.float32), axis=0)
-
-    key_all = total(keys) * scale.reshape(length, 1)
-    value_all = (total(values) * scale.reshape(length, 1)).astype(jnp.bfloat16)
-    query_all = total(query) * row_scale[:, None]
+    summed = jnp.sum(parts.astype(jnp.float32), axis=0)
+    key_all = summed[:, :half, :HEAD_DIM].reshape(length, HEAD_DIM) * scale.reshape(length, 1)
+    value_all = summed[:, :half, HEAD_DIM:].reshape(length, HEAD_DIM) * scale.reshape(length, 1)
+    value_all = value_all.astype(jnp.bfloat16)
+    query_all = summed[:, half:].reshape(seq * CAP, -1) * row_scale[:, None]
     group = query_all.shape[1] // HEAD_DIM
     key_all = rotate(key_all[:, None, :], offsets)[:, 0].astype(jnp.bfloat16)
     query_all = rotate(query_all.reshape(seq * CAP, group, HEAD_DIM), row_pos - row_start).astype(
@@ -583,7 +638,7 @@
     def shards(*args):
         seq, tp = mesh.shape["seq"], mesh.shape["tp"]
         own_heads = args[7].shape[2] // HEAD_DIM
-        moves = tp == 2 and seq == 4 and own_heads % seq == 0
+        moves = tp == 2 and seq == 4 and own_heads == seq and args[6].shape[2] == 2 * args[7].shape[2]
         return (moved_rows if moves else gathered_weights)(*args)
 
     return jax.shard_map(

time: 227 us -> 184 us (0.81)
  Pallas kernels: 170 us -> 143 us
  matrix products: 18.5 us -> 10.6 us
  other arithmetic: 23.7 us -> 17.8 us
  local copies, waits for them, and re-layouts: 9.42 us -> 6.1 us
  starting transfers between devices: 0.07 us -> 2.88 us
    pallas_call x2 -> x1, Pallas kernels: 121 us -> 95.2 us  [project(): pl.pallas_call(functools.partial(project_kernel, seq, pick), out_shape=(j...]
    dot_general x3 -> x0, matrix products: 7.63 us -> none  [the longest x1 4.25 us: moved_rows(): jnp.dot(token_block, w_value[0], preferred_element_type=jnp.float32)]
    slice x3, local copies, waits for them, and re-layouts: 4.22 us -> 0.98 us  [the longest x1 0.9 us: moved_rows(): summed[:, :half, HEAD_DIM:].reshape(length, HEAD_DIM)]
    ppermute x1, starting transfers between devices: 0.07 us -> 2.88 us  [moved_rows(): lax.ppermute(away, 'tp', [(0, 1), (1, 0)]).astype(jnp.float32)]
where the time goes in v2:
time: 184 us; the launch traced here: 183 us
  Pallas kernels  143 us (78%)
  other arithmetic  17.8 us (10%)
  matrix products  10.6 us (6%)
  local copies, waits for them, and re-layouts  6.1 us (3%)
  starting transfers between devices  2.88 us (2%)
  waiting for transfers between devices  2.17 us (1%)
    pallas_call x1, Pallas kernels, project(): pl.pallas_call(functools.partial(project_kernel, seq, pick), out_shape=(j...  95.2 us
    pallas_call x1, Pallas kernels, gather_rows(): pl.pallas_call(functools.partial(rows_kernel, seq), out_shape=(jax.ShapeD...  19.4 us
    pallas_call x1, Pallas kernels, gather_heads(): pl.pallas_call(functools.partial(heads_kernel, seq), out_shape=jax.ShapeD...  18.4 us
    pallas_call x1, Pallas kernels, gather_stats(): pl.pallas_call(functools.partial(stats_kernel, seq), out_shape=jax.ShapeD...  9.95 us
  transfers between devices with their start and end apart: 1, of which 1 were waited for; matrix products, arithmetic and copies ran while one was open for 0% of the time, Pallas kernels for 0%

profile of v2, /device:TPU:0, one launch (start us, length us, event | category | flops | bytes accessed | tf_op | source)
XLA Modules:
  0.0 182.9 jit_solution(2900436908216223635)
XLA Ops:
  0.0 0.0 copy-start
  0.0 0.8 broadcast_compare_fusion.1
  0.8 0.7 convert_element_type.99
  1.6 1.0 reduce-window.15
  2.6 0.1 slice.65
  2.7 0.1 slice_reduce_fusion.1
  2.8 0.1 add_bitcast_fusion.1
  2.9 1.5 fusion.4
  4.4 0.7 constant_dynamic-slice_fusion.3
  5.1 1.5 convolution_convert_fusion
  6.6 0.0 copy-done.1
  6.6 0.3 convolution_convert_fusion.1
  6.9 0.2 fusion.5
  7.2 0.0 copy-done.3
  7.2 0.0 copy-done.4
  7.2 1.2 pad_maximum_fusion.big
  8.4 0.6 select_maximum_fusion.meta
  9.0 95.2 %shard_map.109 = (bf16[4,8,144,256]{3,2,1,0:T(8,128)(2,1)}, bf16[4,2,16,1024]{3,2,1,0:T(8,128)(2,1)}, f32[4,2,8,256]{3,2,1,0:T(8,128)}) custom-call(bf16[2,160,2048]{2,1,0:T(8,128)(2,1)} %pad_maximum_fusion.big, f32[8,256]{1,0:T(8,128)} %select_maximum_fusion.meta, bf16[1024,1024]{1,0:T(8,128)(2,1)} %bitcast.94, bf16[1024,512]{1,0:T(8,128)(2,1)} %bitcast.97, ...), custom_call_target="tpu_custom_call" | custom-call | tf_op jit(solution)/shard_map/pallas_call | solution.py:387
  104.2 0.8 convert_bitcast_fusion
  105.0 0.8 add_rsqrt_fusion
  105.8 0.1 select_reduce_fusion.7
  105.9 0.1 select_reduce_fusion.6
  106.0 2.2 %convert_reduce_fusion = f32[8,144,256]{2,1,0:T(8,128)S(1)} fusion(bf16[4,8,144,256]{3,2,1,0:T(8,128)(2,1)} %get-tuple-element.10), kind=kLoop, calls=%fused_computation.1 | loop fusion | flops 2064384 | bytes 3538944 | tf_op jit(solution)/shard_map/reduce_sum | solution.py:575
  108.2 0.9 fusion.48
  109.1 1.2 reduce-window.19
  110.3 0.1 slice.88
  110.4 0.1 copy.33
  110.5 0.1 copy.34
  110.6 0.1 add_bitcast_fusion
  110.7 0.3 select_reduce_fusion.1
  111.0 0.1 ge.17
  111.1 0.1 le.24
  111.2 0.2 fusion.20
  111.4 0.1 select_reduce_fusion.2
  111.5 0.1 mul.212
  111.6 0.1 reshape.450
  111.6 1.2 copy.43
  112.9 0.3 multiply_cosine_fusion.1
  113.2 0.1 copy_multiply_fusion
  113.3 1.2 fusion.26
  114.5 0.1 subtract_convert_fusion
  114.6 1.4 fusion.11
  116.0 0.7 fusion.50
  116.7 0.2 copy.32
  116.9 2.0 %convolution_convert_fusion.2 = bf16[128,2,128]{2,0,1:T(8,128)(2,1)S(1)} fusion(f32[2,128]{1,0:T(2,128)S(1)} %fusion.50, f32[1024,128]{0,1:T(8,128)S(1)} %copy.32, f32[1024]{0:T(1024)S(1)} %bitcast.107, f32[2,128,1024]{1,2,0:T(8,128)} %fusion.11), kind=kOutput, calls=%fused_computation.21 | convolution fusion | flops 68191488 | bytes 1643520 | tf_op jit(solution)/shard_map/gck,kd->cgd/dot_general | solution.py:592
  118.9 0.7 copy.45.part
  119.6 18.4 %shard_map.110 = bf16[128,1024]{1,0:T(8,128)(2,1)} custom-call(bf16[128,256]{1,0:T(8,128)(2,1)} %copy.45.part), custom_call_target="tpu_custom_call" | custom-call | tf_op jit(solution)/shard_map/pallas_call | solution.py:427
  138.1 1.4 fusion.6
  139.5 2.9 %collective-permute-start = (bf16[64,1024]{1,0:T(8,128)(2,1)S(1)}, bf16[64,1024]{1,0:T(8,128)(2,1)S(1)}, u32[]{:S(2)}, u32[]{:S(2)}) collective-permute-start(bf16[64,1024]{1,0:T(8,128)(2,1)S(1)} %dynamic-slice_convert_fusion), channel_id=1, source_target_pairs={{0,2},{2,0},{1,3},{3,1},{4,6},{6,4},{5,7},{7,5},{8,10},{10,8},{9,1... | collective-permute-start | bytes 393224 | tf_op jit(solution)/shard_map/ppermute | solution.py:601
  142.4 0.1 eq.87
  142.5 0.7 constant_dynamic-slice_fusion.1
  143.2 2.2 %collective-permute-done = bf16[64,1024]{1,0:T(8,128)(2,1)S(1)} collective-permute-done((bf16[64,1024]{1,0:T(8,128)(2,1)S(1)}, bf16[64,1024]{1,0:T(8,128)(2,1)S(1)}, u32[]{:S(2)}, u32[]{:S(2)}) %collective-permute-start) | collective-permute-done | bytes 131104 | tf_op jit(solution)/shard_map/ppermute | solution.py:601
  145.3 0.0 copy-done.2
  145.4 0.8 multiply_reduce_fusion
  146.2 0.6 pad.13.squares
  146.8 19.4 %shard_map.111 = (bf16[128,4096]{1,0:T(8,128)(2,1)}, f32[4,2,8,128]{3,2,1,0:T(8,128)}) custom-call(bf16[64,1024]{1,0:T(8,128)(2,1)} %get-tuple-element.23.part, f32[8,128]{1,0:T(8,128)} %pad.13.squares), custom_call_target="tpu_custom_call" | custom-call | tf_op jit(solution)/shard_map/pallas_call | solution.py:473
  166.2 0.8 slice_reduce_fusion
  167.0 0.1 rsqrt.31
  167.1 3.3 %fusion.51 = (f32[128]{0:T(128)S(1)}, f32[128,512]{1,0:T(8,128)S(1)}) fusion(f32[128]{0:T(128)S(1)} %rsqrt.31, bf16[128,4096]{1,0:T(8,128)(2,1)} %get-tuple-element.13, bf16[1,4096,512]{2,1,0:T(8,128)(2,1)} %param.21), kind=kOutput, calls=%fused_computation.116 | convolution fusion | flops 537001856 | bytes 5506048 | tf_op jit(solution)/shard_map/dot_general | solution.py:606
  170.4 0.2 exponential_reduce_fusion
  170.6 0.6 select_maximum_fusion.3.stats
  171.2 10.0 %shard_map.112 = f32[4,2,8,128]{3,2,1,0:T(8,128)} custom-call(f32[8,128]{1,0:T(8,128)} %select_maximum_fusion.3.stats), custom_call_target="tpu_custom_call" | custom-call | tf_op jit(solution)/shard_map/pallas_call | solution.py:494
  181.2 1.0 constant_dynamic-slice_fusion
  182.2 0.7 select_reduce_fusion.5
  (29 shorter events, 0.3 us)
Async XLA Ops:
  0.0 138.1 %copy-start = (bf16[1,1024,1024]{2,1,0:T(8,128)(2,1)S(1)}, bf16[1,1024,1024]{2,1,0:T(8,128)(2,1)}, u32[]{:S(2)}) copy-start(bf16[1,1024,1024]{2,1,0:T(8,128)(2,1)} %param.20) | copy-start | bytes 6291460
  0.0 6.6 %copy-start.1 = (bf16[1,256,2048]{2,1,0:T(8,128)(2,1)S(1)}, bf16[1,256,2048]{2,1,0:T(8,128)(2,1)}, u32[]{:S(2)}) copy-start(bf16[1,256,2048]{2,1,0:T(8,128)(2,1)} %param.11) | copy-start | bytes 3145732
  5.1 2.1 %copy-start.3 = (s32[256]{0:T(256)S(1)}, s32[256]{0:T(256)}, u32[]{:S(2)}) copy-start(s32[256]{0:T(256)} %param.12) | copy-start | bytes 3076
  5.1 2.1 %copy-start.4 = (s32[256]{0:T(256)S(1)}, s32[256]{0:T(256)}, u32[]{:S(2)}) copy-start(s32[256]{0:T(256)} %param.13) | copy-start | bytes 3076
  118.9 26.4 %copy-start.2 = (bf16[4,2,16,1024]{3,2,1,0:T(8,128)(2,1)S(1)}, bf16[4,2,16,1024]{3,2,1,0:T(8,128)(2,1)}, u32[]{:S(2)}) copy-start(bf16[4,2,16,1024]{3,2,1,0:T(8,128)(2,1)} %get-tuple-element.12) | copy-start | bytes 786436
  139.5 5.8 %collective-permute-start = (bf16[64,1024]{1,0:T(8,128)(2,1)S(1)}, bf16[64,1024]{1,0:T(8,128)(2,1)S(1)}, u32[]{:S(2)}, u32[]{:S(2)}) collective-permute-start(bf16[64,1024]{1,0:T(8,128)(2,1)S(1)} %dynamic-slice_convert_fusion), channel_id=1, source_target_pairs={{0,2},{2,0},{1,3},{3,1},{4,6},{6,4},{5,7},{7,5},{8,10},{10,8},{9,1... | collective-permute-start | bytes 393224 | tf_op jit(solution)/shard_map/ppermute | solution.py:601

commit v3 on v2

--- a/solution.py
+++ b/solution.py
@@ -251,6 +251,7 @@
     half,
     blocks,
     parts,
+    joins,
     send,
     recv,
     fsend,
@@ -308,14 +309,32 @@
             blocks.at[source, t], blocks.at[source, t], fsend.at[source], frecv.at[source], beside
         )
 
-    def handed(chunk, d):
+    side_of = s // 2
+    partner = s + 1 - 2 * lax.rem(s, 2)
+    toward = lax.rem(partner - s + seq, seq)
+
+    def handed(chunk, kind):
+        slot = (0, toward, 2, seq - toward)[kind]
+        target = out.at[kind, chunk] if kind < 3 else joins.at[chunk]
+        peer = lax.rem(s + 2, seq) if kind == 2 else partner
         return remote(
-            parts.at[chunk, d],
-            out.at[d, chunk],
-            psend.at[chunk, d],
-            precv.at[chunk, d],
-            {"seq": lax.rem(s + d, seq), "tp": t},
+            parts.at[chunk, slot],
+            target,
+            psend.at[chunk, kind],
+            precv.at[chunk, kind],
+            {"seq": peer, "tp": t},
         )
+
+    def combine(source):
+        def one(side, carry):
+            chunk = source * 2 + lax.rem(t + side, 2)
+            handed(chunk, 3).wait_recv()
+            both = parts[chunk, 2].astype(jnp.float32) + joins[chunk].astype(jnp.float32)
+            parts[chunk, 2] = both.astype(jnp.bfloat16)
+            handed(chunk, 2).start()
+            return carry
+
+        lax.fori_loop(0, 2, one, 0)
 
     def project(source, side):
         chunk = source * 2 + side
@@ -332,20 +351,20 @@
             place_at[:tokens, :HEAD_DIM] = dot(rows, w_key[:, single]).astype(jnp.bfloat16)
             place_at[:tokens, HEAD_DIM:] = dot(rows, w_value[:, single]).astype(jnp.bfloat16)
             place_at[tokens:] = dot(chosen, w_query[:, double]).astype(jnp.bfloat16)
-        for d in (2, 1, 3):
-            handed(chunk, d).start()
-
-    side_of = s // 2
-    partner = s + 1 - 2 * lax.rem(s, 2)
+        for kind in (3, 1):
+            handed(chunk, kind).start()
+
+    near, far = 2 - side_of, 3 * (1 - side_of)
+
+    def choose(number, first, second, third, fourth):
+        return jnp.where(
+            number == 0,
+            first,
+            jnp.where(number == 1, second, jnp.where(number == 2, third, fourth)),
+        )
 
     def step(number, carry):
-        source = jnp.where(
-            number == 0,
-            s,
-            jnp.where(
-                number == 1, partner, jnp.where(number == 2, 2 - side_of, 3 * (1 - side_of))
-            ),
-        )
+        source = choose(number, s, partner, near, far)
 
         @pl.when(number > 0)
         def _():
@@ -362,9 +381,16 @@
             project(source, which)
             return more
 
-        return lax.fori_loop(0, 2, both, carry)
+        done = lax.fori_loop(0, 2, both, carry)
+
+        @pl.when(number > 0)
+        def _():
+            combine(choose(number, s, partner, s, near))
+
+        return done
 
     lax.fori_loop(0, seq, step, 0)
+    combine(far)
     first.wait_send()
     for source in range(seq):
 
@@ -375,9 +401,10 @@
         passed(source).wait_send()
     for copy in messages:
         copy.wait()
-    for d in range(1, seq):
-        for chunk in range(2 * seq):
-            handed(chunk, d).wait()
+    for chunk in range(2 * seq):
+        for kind in (1, 2):
+            handed(chunk, kind).wait()
+        handed(chunk, 3).wait_send()
 
 
 def project(big, meta, w_query, w_key, w_value, seq, pick):
@@ -387,7 +414,7 @@
     return pl.pallas_call(
         functools.partial(project_kernel, seq, pick),
         out_shape=(
-            jax.ShapeDtypeStruct((seq, 2 * seq, rows - pick, wide), jnp.bfloat16),
+            jax.ShapeDtypeStruct((3, 2 * seq, rows - pick, wide), jnp.bfloat16),
             jax.ShapeDtypeStruct((seq, 2, pick, width), jnp.bfloat16),
             jax.ShapeDtypeStruct((seq, 2) + meta.shape, jnp.float32),
         ),
@@ -397,6 +424,7 @@
             pltpu.VMEM(big.shape[1:], jnp.bfloat16),
             pltpu.VMEM((seq, 2, rows, width), jnp.bfloat16),
             pltpu.VMEM((2 * seq, seq, rows - pick, wide), jnp.bfloat16),
+            pltpu.VMEM((2 * seq, rows - pick, wide), jnp.bfloat16),
         ]
         + [pltpu.SemaphoreType.DMA((seq,))] * 4
         + [pltpu.SemaphoreType.DMA((2 * seq,))] * 2

time: 184 us -> 165 us (0.90)
  Pallas kernels: 143 us -> 126 us
  starting transfers between devices: 2.88 us -> 0.07 us
  waiting for transfers between devices: 2.17 us -> 4.16 us
    pallas_call x1, Pallas kernels: 95.2 us -> 84.9 us  [project(): pl.pallas_call(functools.partial(project_kernel, seq, pick), out_shape=(j...]
    pallas_call x1, Pallas kernels: 18.4 us -> 12 us  [gather_heads(): pl.pallas_call(functools.partial(heads_kernel, seq), out_shape=jax.ShapeD...]
    ppermute x1, starting transfers between devices: 2.88 us -> 0.07 us  [moved_rows(): lax.ppermute(away, 'tp', [(0, 1), (1, 0)]).astype(jnp.float32)]
    ppermute x1, waiting for transfers between devices: 2.17 us -> 4.16 us  [moved_rows(): lax.ppermute(away, 'tp', [(0, 1), (1, 0)]).astype(jnp.float32)]
where the time goes in v3:
time: 165 us; the launch traced here: 164 us
  Pallas kernels  126 us (76%)
  other arithmetic  17.6 us (11%)
  matrix products  10.6 us (6%)
  local copies, waits for them, and re-layouts  6.1 us (4%)
  waiting for transfers between devices  4.16 us (3%)
    pallas_call x1, Pallas kernels, project(): pl.pallas_call(functools.partial(project_kernel, seq, pick), out_shape=(j...  84.9 us
    pallas_call x1, Pallas kernels, gather_rows(): pl.pallas_call(functools.partial(rows_kernel, seq), out_shape=(jax.ShapeD...  19 us
    pallas_call x1, Pallas kernels, gather_heads(): pl.pallas_call(functools.partial(heads_kernel, seq), out_shape=jax.ShapeD...  12 us
    pallas_call x1, Pallas kernels, gather_stats(): pl.pallas_call(functools.partial(stats_kernel, seq), out_shape=jax.ShapeD...  9.7 us
    ppermute x1, waiting for transfers between devices, moved_rows(): lax.ppermute(away, 'tp', [(0, 1), (1, 0)]).astype(jnp.float32)  4.16 us
    another operation x6, other arithmetic  3.52 us
    dot_general x1, matrix products, moved_rows(): logits = jnp.dot(final, head[0], preferred_element_type=jnp.float32)  3.31 us
  transfers between devices with their start and end apart: 1, of which 1 were waited for; matrix products, arithmetic and copies ran while one was open for 0% of the time, Pallas kernels for 0%

profile of v3, /device:TPU:0, one launch (start us, length us, event | category | flops | bytes accessed | tf_op | source)
XLA Modules:
  0.0 164.3 jit_solution(2311115626063322874)
XLA Ops:
  0.0 0.0 copy-start
  0.0 0.8 broadcast_compare_fusion.1
  0.8 0.7 convert_element_type.99
  1.6 1.0 reduce-window.15
  2.6 0.1 slice.65
  2.7 0.1 slice_reduce_fusion.1
  2.8 0.1 add_bitcast_fusion.1
  2.9 1.5 fusion.4
  4.4 0.7 constant_dynamic-slice_fusion.3
  5.1 1.5 convolution_convert_fusion
  6.6 0.0 copy-done.1
  6.6 0.3 convolution_convert_fusion.1
  6.9 0.2 fusion.5
  7.2 0.0 copy-done.3
  7.2 0.0 copy-done.4
  7.2 1.1 pad_maximum_fusion.big
  8.4 0.6 select_maximum_fusion.meta
  9.0 84.9 %shard_map.109 = (bf16[3,8,144,256]{3,2,1,0:T(8,128)(2,1)}, bf16[4,2,16,1024]{3,2,1,0:T(8,128)(2,1)}, f32[4,2,8,256]{3,2,1,0:T(8,128)}) custom-call(bf16[2,160,2048]{2,1,0:T(8,128)(2,1)} %pad_maximum_fusion.big, f32[8,256]{1,0:T(8,128)} %select_maximum_fusion.meta, bf16[1024,1024]{1,0:T(8,128)(2,1)} %bitcast.94, bf16[1024,512]{1,0:T(8,128)(2,1)} %bitcast.97, ...), custom_call_target="tpu_custom_call" | custom-call | tf_op jit(solution)/shard_map/pallas_call | solution.py:414
  93.8 0.8 convert_bitcast_fusion
  94.7 0.8 add_rsqrt_fusion
  95.5 0.1 select_reduce_fusion.7
  95.6 0.1 select_reduce_fusion.6
  95.7 1.9 %convert_reduce_fusion = f32[8,144,256]{2,1,0:T(8,128)S(1)} fusion(bf16[3,8,144,256]{3,2,1,0:T(8,128)(2,1)} %get-tuple-element.10), kind=kLoop, calls=%fused_computation.3 | loop fusion | flops 1474560 | bytes 2949120 | tf_op jit(solution)/shard_map/reduce_sum | solution.py:603
  97.6 0.9 fusion.48
  98.5 1.2 reduce-window.19
  99.7 0.1 slice.88
  99.8 0.1 copy.33
  99.9 0.1 copy.34
  100.0 0.1 add_bitcast_fusion
  100.1 0.3 select_reduce_fusion.1
  100.4 0.1 ge.17
  100.5 0.1 le.24
  100.6 0.2 fusion.20
  100.8 0.1 select_reduce_fusion.2
  100.9 0.1 mul.212
  101.0 0.1 reshape.450
  101.0 1.2 copy.43
  102.3 0.3 multiply_cosine_fusion.1
  102.6 0.1 copy_multiply_fusion
  102.7 1.2 fusion.26
  103.9 0.1 subtract_convert_fusion
  104.0 1.4 fusion.11
  105.4 0.7 fusion.50
  106.1 0.2 copy.32
  106.3 2.0 %convolution_convert_fusion.2 = bf16[128,2,128]{2,0,1:T(8,128)(2,1)S(1)} fusion(f32[2,128]{1,0:T(2,128)S(1)} %fusion.50, f32[1024,128]{0,1:T(8,128)S(1)} %copy.32, f32[1024]{0:T(1024)S(1)} %bitcast.107, f32[2,128,1024]{1,2,0:T(8,128)} %fusion.11), kind=kOutput, calls=%fused_computation.21 | convolution fusion | flops 68191488 | bytes 1643520 | tf_op jit(solution)/shard_map/gck,kd->cgd/dot_general | solution.py:620
  108.3 0.0 copy-start.2
  108.3 0.7 copy.45.part
  109.1 12.0 %shard_map.110 = bf16[128,1024]{1,0:T(8,128)(2,1)} custom-call(bf16[128,256]{1,0:T(8,128)(2,1)} %copy.45.part), custom_call_target="tpu_custom_call" | custom-call | tf_op jit(solution)/shard_map/pallas_call | solution.py:455
  121.0 1.4 fusion.6
  122.5 0.1 collective-permute-start
  122.6 0.1 eq.87
  122.7 0.7 constant_dynamic-slice_fusion.1
  123.3 4.2 %collective-permute-done = bf16[64,1024]{1,0:T(8,128)(2,1)S(1)} collective-permute-done((bf16[64,1024]{1,0:T(8,128)(2,1)S(1)}, bf16[64,1024]{1,0:T(8,128)(2,1)S(1)}, u32[]{:S(2)}, u32[]{:S(2)}) %collective-permute-start) | collective-permute-done | bytes 131104 | tf_op jit(solution)/shard_map/ppermute | solution.py:629
  127.5 0.8 multiply_reduce_fusion
  128.3 0.6 pad.13.squares
  128.9 19.0 %shard_map.111 = (bf16[128,4096]{1,0:T(8,128)(2,1)}, f32[4,2,8,128]{3,2,1,0:T(8,128)}) custom-call(bf16[64,1024]{1,0:T(8,128)(2,1)} %get-tuple-element.23.part, f32[8,128]{1,0:T(8,128)} %pad.13.squares), custom_call_target="tpu_custom_call" | custom-call | tf_op jit(solution)/shard_map/pallas_call | solution.py:501
  147.9 0.8 slice_reduce_fusion
  148.7 0.1 rsqrt.31
  148.8 3.3 %fusion.51 = (f32[128]{0:T(128)S(1)}, f32[128,512]{1,0:T(8,128)S(1)}) fusion(f32[128]{0:T(128)S(1)} %rsqrt.31, bf16[128,4096]{1,0:T(8,128)(2,1)} %get-tuple-element.13, bf16[1,4096,512]{2,1,0:T(8,128)(2,1)} %param.21), kind=kOutput, calls=%fused_computation.116 | convolution fusion | flops 537001856 | bytes 5506048 | tf_op jit(solution)/shard_map/dot_general | solution.py:634
  152.1 0.2 exponential_reduce_fusion
  152.3 0.6 select_maximum_fusion.3.stats
  152.9 9.7 %shard_map.112 = f32[4,2,8,128]{3,2,1,0:T(8,128)} custom-call(f32[8,128]{1,0:T(8,128)} %select_maximum_fusion.3.stats), custom_call_target="tpu_custom_call" | custom-call | tf_op jit(solution)/shard_map/pallas_call | solution.py:522
  162.6 1.0 constant_dynamic-slice_fusion
  163.7 0.7 select_reduce_fusion.5
  (29 shorter events, 0.3 us)
Async XLA Ops:
  0.0 121.0 %copy-start = (bf16[1,1024,1024]{2,1,0:T(8,128)(2,1)S(1)}, bf16[1,1024,1024]{2,1,0:T(8,128)(2,1)}, u32[]{:S(2)}) copy-start(bf16[1,1024,1024]{2,1,0:T(8,128)(2,1)} %param.20) | copy-start | bytes 6291460
  0.0 6.6 %copy-start.1 = (bf16[1,256,2048]{2,1,0:T(8,128)(2,1)S(1)}, bf16[1,256,2048]{2,1,0:T(8,128)(2,1)}, u32[]{:S(2)}) copy-start(bf16[1,256,2048]{2,1,0:T(8,128)(2,1)} %param.11) | copy-start | bytes 3145732
  5.1 2.1 %copy-start.3 = (s32[256]{0:T(256)S(1)}, s32[256]{0:T(256)}, u32[]{:S(2)}) copy-start(s32[256]{0:T(256)} %param.12) | copy-start | bytes 3076
  5.1 2.1 %copy-start.4 = (s32[256]{0:T(256)S(1)}, s32[256]{0:T(256)}, u32[]{:S(2)}) copy-start(s32[256]{0:T(256)} %param.13) | copy-start | bytes 3076
  108.3 19.2 %copy-start.2 = (bf16[4,2,16,1024]{3,2,1,0:T(8,128)(2,1)S(1)}, bf16[4,2,16,1024]{3,2,1,0:T(8,128)(2,1)}, u32[]{:S(2)}) copy-start(bf16[4,2,16,1024]{3,2,1,0:T(8,128)(2,1)} %get-tuple-element.12) | copy-start | bytes 786436
  122.5 5.0 %collective-permute-start = (bf16[64,1024]{1,0:T(8,128)(2,1)S(1)}, bf16[64,1024]{1,0:T(8,128)(2,1)S(1)}, u32[]{:S(2)}, u32[]{:S(2)}) collective-permute-start(bf16[64,1024]{1,0:T(8,128)(2,1)S(1)} %dynamic-slice_convert_fusion), channel_id=1, source_target_pairs={{0,2},{2,0},{1,3},{3,1},{4,6},{6,4},{5,7},{7,5},{8,10},{10,8},{9,1... | collective-permute-start | bytes 393224 | tf_op jit(solution)/shard_map/ppermute | solution.py:629
